TPU v7x, 256 devices: a whole 4x4x8 slice. The times are simulated.
256 devices in a mesh: trial: 2 (over core), qa: 16 (over y, x), qb: 8 (over z).
Axes of the slice: x: 4, y: 4, z: 8, core: 2. Of those that a mesh axis runs over, the one named last changes fastest.
Arguments:
- wave_parts: float32 [4, 512, 128, 128], P('trial', ('qa', 'qb')), parts along dimension 0, may hold values from -6 to 6
- level_table: float32 [1024, 128, 128], P(('trial', 'qa', 'qb')), parts along dimension 0, may hold values from -2 to 2
- diagonal_angles: float32 [6, 128], P('trial'), parts along dimension 0, may hold values from 0.3 to 1.2
- turn_angles: float32 [6, 4], P('trial'), parts along dimension 0, may hold values from 0.3 to 1.2
Outputs:
- final_parts: float32 [4, 512, 128, 128], P('trial', ('qa', 'qb')), parts along dimension 0
There are 2 independent parts, one for each index of `trial`. A program takes and returns all parts, laid end to end along the dimension named above; each array names one. Nothing has to cross between parts.
All inputs are finite; a program needn't handle non-finite values.
Results may differ from a plain program's by a relative error of at most 0.0003.
Values sent between devices are 32-bit elements.
No kernel may reach another device: no remote copies, remote signals or barrier semaphores. Data moves between devices by JAX's collectives and lax.ppermute only.
A program may use at most 64 MiB of HBM per device.

v0:
```python
import jax
import jax.numpy as jnp
from jax import lax
from jax.sharding import PartitionSpec as P

LAYERS = 3


def count_bits(values, count):
    places = jnp.arange(count.bit_length() - 1, dtype=jnp.int32)
    return jnp.sum(values[..., None] >> places & 1, axis=-1)


def rotation_table(count, angle):
    rank = jnp.arange(count, dtype=jnp.int32)
    apart = count_bits(rank[:, None] ^ rank[None, :], count)
    bits = count.bit_length() - 1
    size = jnp.cos(angle) ** (bits - apart).astype(jnp.float32) * jnp.sin(angle) ** apart.astype(
        jnp.float32
    )
    real_sign = jnp.where(apart % 4 == 0, 1.0, jnp.where(apart % 4 == 2, -1.0, 0.0)).astype(
        jnp.float32
    )
    imag_sign = jnp.where(apart % 4 == 1, -1.0, jnp.where(apart % 4 == 3, 1.0, 0.0)).astype(
        jnp.float32
    )
    return (size * real_sign, size * imag_sign)


def mix_dim(values, dim, angle):
    real_part, imag_part = rotation_table(values.shape[dim], angle)

    def times(table):
        moved = jnp.tensordot(values, table, axes=([dim], [0]), precision=lax.Precision.HIGHEST)
        return jnp.moveaxis(moved, -1, dim)

    by_real = times(real_part)
    by_imag = times(imag_part)
    return jnp.stack([by_real[0] - by_imag[1], by_real[1] + by_imag[0]])


def phase_step(values, levels, angle):
    turn = angle * levels
    return jnp.stack(
        [
            values[0] * jnp.cos(turn) + values[1] * jnp.sin(turn),
            values[1] * jnp.cos(turn) - values[0] * jnp.sin(turn),
        ]
    )


def shards(wave_parts, level_table, diagonal_angles, turn_angles):
    values = wave_parts
    for layer in range(LAYERS):
        values = phase_step(values, level_table, diagonal_angles[layer])
        values = mix_dim(values, 3, turn_angles[layer, 0])
        values = mix_dim(values, 2, turn_angles[layer, 1])
        moved = lax.all_to_all(values, "qa", split_axis=2, concat_axis=1, tiled=True)
        moved = mix_dim(moved, 1, turn_angles[layer, 2])
        values = lax.all_to_all(moved, "qa", split_axis=1, concat_axis=2, tiled=True)
        moved = lax.all_to_all(values, "qb", split_axis=3, concat_axis=1, tiled=True)
        spread = moved.reshape(2, lax.axis_size("qb"), -1, moved.shape[2], moved.shape[3])
        moved = mix_dim(spread, 1, turn_angles[layer, 3]).reshape(moved.shape)
        values = lax.all_to_all(moved, "qb", split_axis=1, concat_axis=3, tiled=True)
    return values


def solution(mesh):
    placed = (
        P("trial", ("qa", "qb"), None, None),
        P(("trial", "qa", "qb"), None, None),
        P("trial", None),
        P("trial", None),
    )
    return jax.shard_map(
        shards,
        mesh=mesh,
        in_specs=placed,
        out_specs=P("trial", ("qa", "qb"), None, None),
        check_vma=False,
    )
```

profile of v0, /device:TPU:32, one launch (start us, length us, event | category | flops | bytes accessed | tf_op | source)
XLA Modules:
  0.0 244.3 jit_solution(5712961371041318198)
XLA Ops:
  0.0 1.8 fusion.327
  3.8 2.0 fusion.19
  9.0 1.1 convolution_bitcast_fusion.17
  10.1 1.1 convolution_bitcast_fusion.16
  11.3 1.0 copy.169
  12.3 7.0 %all-to-all-start = ((f32[2,4,128,128]{3,1,0,2:T(4,128)}), f32[2,4,128,128]{3,1,0,2:T(4,128)S(1)}, u32[]{:S(2)}, u32[]{:S(2)}) async-start(f32[2,4,128,128]{3,1,0,2:T(4,128)} %copy.169), calls=%async_computation | async-start | bytes 1048576 | tf_op jit(solution)/shard_map/all_to_all | solution.py:58
  20.9 10.6 %all-to-all-done = f32[2,4,128,128]{3,1,0,2:T(4,128)S(1)} async-done(((f32[2,4,128,128]{3,1,0,2:T(4,128)}), f32[2,4,128,128]{3,1,0,2:T(4,128)S(1)}, u32[]{:S(2)}, u32[]{:S(2)}) %all-to-all-start) | async-done | bytes 524320 | tf_op jit(solution)/shard_map/all_to_all | solution.py:58
  33.8 13.4 %all_to_all.201 = f32[2,64,8,128]{3,2,0,1:T(8,128)S(1)} all-to-all(f32[2,64,8,128]{3,2,0,1:T(8,128)S(1)} %copy.174), channel_id=1, replica_groups=mesh['trial'=2,'qa'=16,'qb'=8] {'qa'}, dimensions={1} | all-to-all | bytes 1048576 | tf_op jit(solution)/shard_map/all_to_all | solution.py:60
  47.3 1.0 copy.177
  48.3 8.6 %all-to-all-start.2 = ((f32[2,4,128,128]{2,1,0,3:T(4,128)}), f32[2,4,128,128]{2,1,0,3:T(4,128)S(1)}, u32[]{:S(2)}, u32[]{:S(2)}) async-start(f32[2,4,128,128]{2,1,0,3:T(4,128)} %copy.177), calls=%async_computation.2 | async-start | bytes 1048576 | tf_op jit(solution)/shard_map/all_to_all | solution.py:61
  58.4 12.7 %all-to-all-done.2 = f32[2,4,128,128]{2,1,0,3:T(4,128)S(1)} async-done(((f32[2,4,128,128]{2,1,0,3:T(4,128)}), f32[2,4,128,128]{2,1,0,3:T(4,128)S(1)}, u32[]{:S(2)}, u32[]{:S(2)}) %all-to-all-start.2) | async-done | bytes 524320 | tf_op jit(solution)/shard_map/all_to_all | solution.py:61
  73.9 4.7 %all-to-all-start.3 = ((f32[2,32,128,16]{2,3,0,1:T(8,128)}), f32[2,32,128,16]{2,3,0,1:T(8,128)S(1)}, u32[]{:S(2)}, u32[]{:S(2)}) async-start(f32[2,32,128,16]{2,3,0,1:T(8,128)} %copy.184), calls=%async_computation.3 | async-start | bytes 1048576 | tf_op jit(solution)/shard_map/all_to_all | solution.py:64
  81.2 10.7 %all-to-all-done.3 = f32[2,32,128,16]{2,3,0,1:T(8,128)S(1)} async-done(((f32[2,32,128,16]{2,3,0,1:T(8,128)}), f32[2,32,128,16]{2,3,0,1:T(8,128)S(1)}, u32[]{:S(2)}, u32[]{:S(2)}) %all-to-all-start.3) | async-done | bytes 524320 | tf_op jit(solution)/shard_map/all_to_all | solution.py:64
  93.2 1.0 add_bitcast_fusion.1
  95.8 1.1 convolution_bitcast_fusion.11
  96.9 1.1 convolution_bitcast_fusion.10
  99.1 4.9 %all-to-all-start.4 = ((f32[2,4,128,128]{3,1,0,2:T(4,128)}), f32[2,4,128,128]{3,1,0,2:T(4,128)S(1)}, u32[]{:S(2)}, u32[]{:S(2)}) async-start(f32[2,4,128,128]{3,1,0,2:T(4,128)} %copy.194), calls=%async_computation.4 | async-start | bytes 1048576 | tf_op jit(solution)/shard_map/all_to_all | solution.py:58
  105.4 8.7 %all-to-all-done.4 = f32[2,4,128,128]{3,1,0,2:T(4,128)S(1)} async-done(((f32[2,4,128,128]{3,1,0,2:T(4,128)}), f32[2,4,128,128]{3,1,0,2:T(4,128)S(1)}, u32[]{:S(2)}, u32[]{:S(2)}) %all-to-all-start.4) | async-done | bytes 524320 | tf_op jit(solution)/shard_map/all_to_all | solution.py:58
  116.5 12.7 %all_to_all.202 = f32[2,64,8,128]{3,2,0,1:T(8,128)S(1)} all-to-all(f32[2,64,8,128]{3,2,0,1:T(8,128)S(1)} %copy.199), channel_id=1, replica_groups=mesh['trial'=2,'qa'=16,'qb'=8] {'qa'}, dimensions={1} | all-to-all | bytes 1048576 | tf_op jit(solution)/shard_map/all_to_all | solution.py:60
  130.3 5.3 %all-to-all-start.6 = ((f32[2,4,128,128]{2,1,0,3:T(4,128)}), f32[2,4,128,128]{2,1,0,3:T(4,128)S(1)}, u32[]{:S(2)}, u32[]{:S(2)}) async-start(f32[2,4,128,128]{2,1,0,3:T(4,128)} %copy.202), calls=%async_computation.6 | async-start | bytes 1048576 | tf_op jit(solution)/shard_map/all_to_all | solution.py:61
  136.9 12.6 %all-to-all-done.6 = f32[2,4,128,128]{2,1,0,3:T(4,128)S(1)} async-done(((f32[2,4,128,128]{2,1,0,3:T(4,128)}), f32[2,4,128,128]{2,1,0,3:T(4,128)S(1)}, u32[]{:S(2)}, u32[]{:S(2)}) %all-to-all-start.6) | async-done | bytes 524320 | tf_op jit(solution)/shard_map/all_to_all | solution.py:61
  152.4 4.8 %all-to-all-start.7 = ((f32[2,32,128,16]{2,3,0,1:T(8,128)}), f32[2,32,128,16]{2,3,0,1:T(8,128)S(1)}, u32[]{:S(2)}, u32[]{:S(2)}) async-start(f32[2,32,128,16]{2,3,0,1:T(8,128)} %copy.209), calls=%async_computation.7 | async-start | bytes 1048576 | tf_op jit(solution)/shard_map/all_to_all | solution.py:64
  160.1 9.5 %all-to-all-done.7 = f32[2,32,128,16]{2,3,0,1:T(8,128)S(1)} async-done(((f32[2,32,128,16]{2,3,0,1:T(8,128)}), f32[2,32,128,16]{2,3,0,1:T(8,128)S(1)}, u32[]{:S(2)}, u32[]{:S(2)}) %all-to-all-start.7) | async-done | bytes 524320 | tf_op jit(solution)/shard_map/all_to_all | solution.py:64
  170.0 1.0 add_bitcast_fusion
  172.6 1.1 convolution_bitcast_fusion.5
  173.7 1.1 convolution_bitcast_fusion.4
  176.0 6.2 %all-to-all-start.8 = ((f32[2,4,128,128]{3,1,0,2:T(4,128)}), f32[2,4,128,128]{3,1,0,2:T(4,128)S(1)}, u32[]{:S(2)}, u32[]{:S(2)}) async-start(f32[2,4,128,128]{3,1,0,2:T(4,128)} %copy.219), calls=%async_computation.8 | async-start | bytes 1048576 | tf_op jit(solution)/shard_map/all_to_all | solution.py:58
  183.6 8.7 %all-to-all-done.8 = f32[2,4,128,128]{3,1,0,2:T(4,128)S(1)} async-done(((f32[2,4,128,128]{3,1,0,2:T(4,128)}), f32[2,4,128,128]{3,1,0,2:T(4,128)S(1)}, u32[]{:S(2)}, u32[]{:S(2)}) %all-to-all-start.8) | async-done | bytes 524320 | tf_op jit(solution)/shard_map/all_to_all | solution.py:58
  194.6 12.8 %all_to_all.203 = f32[2,64,8,128]{3,2,0,1:T(8,128)S(1)} all-to-all(f32[2,64,8,128]{3,2,0,1:T(8,128)S(1)} %copy.224), channel_id=1, replica_groups=mesh['trial'=2,'qa'=16,'qb'=8] {'qa'}, dimensions={1} | all-to-all | bytes 1048576 | tf_op jit(solution)/shard_map/all_to_all | solution.py:60
  208.4 4.5 %all-to-all-start.10 = ((f32[2,4,128,128]{2,1,0,3:T(4,128)}), f32[2,4,128,128]{2,1,0,3:T(4,128)S(1)}, u32[]{:S(2)}, u32[]{:S(2)}) async-start(f32[2,4,128,128]{2,1,0,3:T(4,128)} %copy.227), calls=%async_computation.10 | async-start | bytes 1048576 | tf_op jit(solution)/shard_map/all_to_all | solution.py:61
  214.4 10.6 %all-to-all-done.10 = f32[2,4,128,128]{2,1,0,3:T(4,128)S(1)} async-done(((f32[2,4,128,128]{2,1,0,3:T(4,128)}), f32[2,4,128,128]{2,1,0,3:T(4,128)S(1)}, u32[]{:S(2)}, u32[]{:S(2)}) %all-to-all-start.10) | async-done | bytes 524320 | tf_op jit(solution)/shard_map/all_to_all | solution.py:61
  227.1 16.2 %all_to_all.204 = f32[2,32,128,16]{2,3,0,1:T(8,128)S(1)} all-to-all(f32[2,32,128,16]{2,3,0,1:T(8,128)S(1)} %copy.234), channel_id=1, replica_groups=mesh['trial'=2,'qa'=16,'qb'=8] {'qb'}, dimensions={1} | all-to-all | bytes 1048576 | tf_op jit(solution)/shard_map/all_to_all | solution.py:64
  (89 shorter events, 27.1 us)
Async XLA Ops:
  3.1 0.7 copy-start.1
  12.3 19.2 %all-to-all-start = ((f32[2,4,128,128]{3,1,0,2:T(4,128)}), f32[2,4,128,128]{3,1,0,2:T(4,128)S(1)}, u32[]{:S(2)}, u32[]{:S(2)}) async-start(f32[2,4,128,128]{3,1,0,2:T(4,128)} %copy.169), calls=%async_computation | async-start | bytes 1048576 | tf_op jit(solution)/shard_map/all_to_all | solution.py:58
  48.3 22.8 %all-to-all-start.2 = ((f32[2,4,128,128]{2,1,0,3:T(4,128)}), f32[2,4,128,128]{2,1,0,3:T(4,128)S(1)}, u32[]{:S(2)}, u32[]{:S(2)}) async-start(f32[2,4,128,128]{2,1,0,3:T(4,128)} %copy.177), calls=%async_computation.2 | async-start | bytes 1048576 | tf_op jit(solution)/shard_map/all_to_all | solution.py:61
  73.9 18.0 %all-to-all-start.3 = ((f32[2,32,128,16]{2,3,0,1:T(8,128)}), f32[2,32,128,16]{2,3,0,1:T(8,128)S(1)}, u32[]{:S(2)}, u32[]{:S(2)}) async-start(f32[2,32,128,16]{2,3,0,1:T(8,128)} %copy.184), calls=%async_computation.3 | async-start | bytes 1048576 | tf_op jit(solution)/shard_map/all_to_all | solution.py:64
  92.2 1.0 copy-start
  99.1 15.0 %all-to-all-start.4 = ((f32[2,4,128,128]{3,1,0,2:T(4,128)}), f32[2,4,128,128]{3,1,0,2:T(4,128)S(1)}, u32[]{:S(2)}, u32[]{:S(2)}) async-start(f32[2,4,128,128]{3,1,0,2:T(4,128)} %copy.194), calls=%async_computation.4 | async-start | bytes 1048576 | tf_op jit(solution)/shard_map/all_to_all | solution.py:58
  130.3 19.3 %all-to-all-start.6 = ((f32[2,4,128,128]{2,1,0,3:T(4,128)}), f32[2,4,128,128]{2,1,0,3:T(4,128)S(1)}, u32[]{:S(2)}, u32[]{:S(2)}) async-start(f32[2,4,128,128]{2,1,0,3:T(4,128)} %copy.202), calls=%async_computation.6 | async-start | bytes 1048576 | tf_op jit(solution)/shard_map/all_to_all | solution.py:61
  152.4 17.2 %all-to-all-start.7 = ((f32[2,32,128,16]{2,3,0,1:T(8,128)}), f32[2,32,128,16]{2,3,0,1:T(8,128)S(1)}, u32[]{:S(2)}, u32[]{:S(2)}) async-start(f32[2,32,128,16]{2,3,0,1:T(8,128)} %copy.209), calls=%async_computation.7 | async-start | bytes 1048576 | tf_op jit(solution)/shard_map/all_to_all | solution.py:64
  176.0 16.3 %all-to-all-start.8 = ((f32[2,4,128,128]{3,1,0,2:T(4,128)}), f32[2,4,128,128]{3,1,0,2:T(4,128)S(1)}, u32[]{:S(2)}, u32[]{:S(2)}) async-start(f32[2,4,128,128]{3,1,0,2:T(4,128)} %copy.219), calls=%async_computation.8 | async-start | bytes 1048576 | tf_op jit(solution)/shard_map/all_to_all | solution.py:58
  208.4 16.6 %all-to-all-start.10 = ((f32[2,4,128,128]{2,1,0,3:T(4,128)}), f32[2,4,128,128]{2,1,0,3:T(4,128)S(1)}, u32[]{:S(2)}, u32[]{:S(2)}) async-start(f32[2,4,128,128]{2,1,0,3:T(4,128)} %copy.227), calls=%async_computation.10 | async-start | bytes 1048576 | tf_op jit(solution)/shard_map/all_to_all | solution.py:61
where the time goes:
time: 246 us; the launch traced here: 244 us
  waiting for transfers between devices  84 us (34%)
  blocking collectives  55.1 us (22%)
  starting transfers between devices  46 us (19%)
  matrix products  20.9 us (8%)
  between operations  17.6 us (7%)
  local copies, waits for them, and re-layouts  15.4 us (6%)
  other arithmetic  5.26 us (2%)
    all_to_all x3, blocking collectives, shards(): lax.all_to_all(moved, 'qa', split_axis=1, concat_axis=2, tiled=True)  38.9 us
    all_to_all x3, waiting for transfers between devices, shards(): lax.all_to_all(values, 'qb', split_axis=3, concat_axis=1, tiled=True)  35.8 us
    all_to_all x3, waiting for transfers between devices, shards(): lax.all_to_all(values, 'qa', split_axis=2, concat_axis=1, tiled=True)  28 us
    dot_general x24, matrix products, times(): jnp.tensordot(values, table, axes=([dim], [0]), precision=lax.Precision.H...  20.9 us
    all_to_all x2, waiting for transfers between devices, shards(): lax.all_to_all(moved, 'qb', split_axis=1, concat_axis=3, tiled=True)  20.2 us
    all_to_all x3, starting transfers between devices, shards(): lax.all_to_all(values, 'qb', split_axis=3, concat_axis=1, tiled=True)  18.5 us
    all_to_all x3, starting transfers between devices, shards(): lax.all_to_all(values, 'qa', split_axis=2, concat_axis=1, tiled=True)  18.1 us
    all_to_all x1, blocking collectives, shards(): lax.all_to_all(moved, 'qb', split_axis=1, concat_axis=3, tiled=True)  16.2 us
  transfers between devices with their start and end apart: 8, of which 8 were waited for; matrix products, arithmetic and copies ran while one was open for 0% of the time, Pallas kernels for 0%

commit v1 on v0

v1 whole, which is shorter than its diff:
```python
import jax
import jax.numpy as jnp
from jax import lax
from jax.sharding import PartitionSpec as P

LAYERS = 3
HIGH = lax.Precision.HIGHEST


def count_bits(values):
    places = jnp.arange(10, dtype=jnp.int32)
    return jnp.sum(values[..., None] >> places & 1, axis=-1)


def rotation(count, angle):
    rank = jnp.arange(count, dtype=jnp.int32)
    to, of = rank[:, None], rank[None, :]
    apart = count_bits(to ^ of)
    bits = count.bit_length() - 1
    size = jnp.cos(angle) ** (bits - apart).astype(jnp.float32) * jnp.sin(angle) ** apart.astype(
        jnp.float32
    )
    return jnp.where(count_bits(to & ~of) % 2 == 0, size, -size)


def quarter_turns(real, imag, turns):
    odd = turns % 2 == 1
    new_real = jnp.where(odd, -imag, real)
    new_imag = jnp.where(odd, real, imag)
    sign = jnp.where(turns % 4 >= 2, -1.0, 1.0).astype(jnp.float32)
    return new_real * sign, new_imag * sign


def phase(real, imag, turn):
    cos, sin = jnp.cos(turn), jnp.sin(turn)
    return real * cos + imag * sin, imag * cos - real * sin


def exchange(values):
    return lax.all_to_all(values, ("qa", "qb"), split_axis=0, concat_axis=0, tiled=True)


def shards(wave_parts, level_table, diagonal_angles, turn_angles):
    n_qa, n_qb = lax.axis_size("qa"), lax.axis_size("qb")
    place = lax.axis_index("qa") * n_qb + lax.axis_index("qb")
    n_q = n_qa * n_qb
    blocks, rows, lanes = level_table.shape
    lane_mix = [rotation(lanes, turn_angles[i, 0]) for i in range(LAYERS)]
    row_mix = [rotation(rows, turn_angles[i, 1]) for i in range(LAYERS)]
    block_mix = [rotation(blocks, turn_angles[i, 2]) for i in range(LAYERS)]
    q_mix = [
        jnp.kron(rotation(n_qa, turn_angles[i, 2]), rotation(n_qb, turn_angles[i, 3]))
        for i in range(LAYERS)
    ]

    turns = (
        count_bits(place)
        + count_bits(jnp.arange(blocks))[:, None, None]
        + count_bits(jnp.arange(rows))[None, :, None]
        + count_bits(jnp.arange(lanes))[None, None, :]
    )

    real, imag = quarter_turns(wave_parts[0], wave_parts[1], -turns % 4)
    real, imag = phase(real, imag, diagonal_angles[0] * level_table)
    values = jnp.stack([real, imag])
    values = jnp.einsum("cbrl,kl->cbrk", values, lane_mix[0], precision=HIGH)
    values = jnp.einsum("cbrk,ab->cark", values, block_mix[0], precision=HIGH)
    values = jnp.einsum("cark,sr->scak", values, row_mix[0], precision=HIGH)
    sent = jnp.concatenate(
        [
            values.reshape(rows, 2 * blocks, lanes),
            jnp.moveaxis(level_table, 1, 0),
            jnp.moveaxis(level_table, 2, 0),
        ],
        axis=1,
    )
    got = exchange(sent)

    values = got[:, : 2 * blocks].reshape(n_q, 2, blocks, lanes)
    by_row, by_lane = got[:, 2 * blocks : 3 * blocks], got[:, 3 * blocks :]
    values = jnp.einsum("pq,qcbl->pcbl", q_mix[0], values, precision=HIGH)
    real, imag = phase(values[:, 0], values[:, 1], diagonal_angles[1] * by_row)
    values = jnp.stack([real, imag], axis=1)
    values = jnp.einsum("pq,qcbl->pcbl", q_mix[1], values, precision=HIGH)
    values = jnp.einsum("ab,qcbl->qcal", block_mix[1], values, precision=HIGH)
    values = jnp.einsum("kl,qcal->kcaq", lane_mix[1], values, precision=HIGH)
    values = exchange(values.reshape(lanes, 2 * blocks, n_q)).reshape(rows, 2, blocks, n_q)

    values = jnp.einsum("sr,rcbq->scbq", row_mix[1], values, precision=HIGH)
    own_angle = lax.dynamic_index_in_dim(diagonal_angles[2], place, 0, keepdims=False)
    real, imag = phase(values[:, 0], values[:, 1], own_angle * jnp.transpose(by_lane, (2, 1, 0)))
    values = jnp.stack([real, imag], axis=1)
    values = jnp.einsum("sr,rcbq->scbq", row_mix[2], values, precision=HIGH)
    values = jnp.einsum("ab,rcbq->rcaq", block_mix[2], values, precision=HIGH)
    values = jnp.einsum("pq,rcaq->pcar", q_mix[2], values, precision=HIGH)
    values = exchange(values.reshape(n_q, 2 * blocks, rows)).reshape(lanes, 2, blocks, rows)

    values = jnp.einsum("kl,lcbr->cbrk", lane_mix[2], values, precision=HIGH)
    real, imag = quarter_turns(values[0], values[1], turns)
    return jnp.stack([real, imag])


def solution(mesh):
    placed = (
        P("trial", ("qa", "qb"), None, None),
        P(("trial", "qa", "qb"), None, None),
        P("trial", None),
        P("trial", None),
    )
    return jax.shard_map(
        shards,
        mesh=mesh,
        in_specs=placed,
        out_specs=P("trial", ("qa", "qb"), None, None),
        check_vma=False,
    )
```

time: 246 us -> 127 us (0.52)
  blocking collectives: 55.1 us -> 0 us
  waiting for transfers between devices: 84 us -> 53.6 us
  starting transfers between devices: 46 us -> 27.8 us
  matrix products: 20.9 us -> 10.2 us
  local copies, waits for them, and re-layouts: 15.4 us -> 9.01 us
  other arithmetic: 5.26 us -> 8.44 us
    all_to_all x4 -> x0, blocking collectives: 55.1 us -> none  [the longest x3 38.9 us: shards(): lax.all_to_all(moved, 'qa', split_axis=1, concat_axis=2, tiled=True)]
    all_to_all x8 -> x3, waiting for transfers between devices: 84 us -> 53.6 us  [exchange(): lax.all_to_all(values, ('qa', 'qb'), split_axis=0, concat_axis=0, tiled=T...]
    all_to_all x8 -> x3, starting transfers between devices: 46 us -> 27.8 us  [exchange(): lax.all_to_all(values, ('qa', 'qb'), split_axis=0, concat_axis=0, tiled=T...]
    dot_general x24 -> x12, matrix products: 20.9 us -> 10.2 us  [the longest x1 1.32 us: shards(): values = jnp.einsum('ab,qcbl->qcal', block_mix[1], values, precision=HIGH)]
    another operation x9 -> x0, local copies, waits for them, and re-layouts: 5.69 us -> none  [mix_dim(): return jnp.stack([by_real[0] - by_imag[1], by_real[1] + by_imag[0]])]
    all_to_all x16 -> x2, local copies, waits for them, and re-layouts: 5.52 us -> 0.33 us  [exchange(): lax.all_to_all(values, ('qa', 'qb'), split_axis=0, concat_axis=0, tiled=T...]
  transfers between devices with their start and end apart: 8 -> 3, of which waited for: 8 -> 3; matrix products, arithmetic and copies ran while one was open for 0% -> 3% of each run, Pallas kernels for 0% -> 0%
where the time goes in v1:
time: 127 us; the launch traced here: 126 us
  waiting for transfers between devices  53.6 us (42%)
  starting transfers between devices  27.8 us (22%)
  between operations  17.1 us (13%)
  matrix products  10.2 us (8%)
  local copies, waits for them, and re-layouts  9.01 us (7%)
  other arithmetic  8.44 us (7%)
    all_to_all x3, waiting for transfers between devices, exchange(): lax.all_to_all(values, ('qa', 'qb'), split_axis=0, concat_axis=0, tiled=T...  53.6 us
    all_to_all x3, starting transfers between devices, exchange(): lax.all_to_all(values, ('qa', 'qb'), split_axis=0, concat_axis=0, tiled=T...  27.8 us
    another operation x2, other arithmetic, shards(): values = jnp.stack([real, imag], axis=1)  2.62 us
  transfers between devices with their start and end apart: 3, of which 3 were waited for; matrix products, arithmetic and copies ran while one was open for 3% of the time, Pallas kernels for 0%

profile of v1, /device:TPU:32, one launch (start us, length us, event | category | flops | bytes accessed | tf_op | source)
XLA Modules:
  0.0 126.1 jit_solution(4623939076734122196)
XLA Ops:
  0.0 1.8 %fusion.168 = (f32[1,1]{1,0:T(1,128)}, f32[1,1]{1,0:T(1,128)}, f32[1,1]{1,0:T(1,128)}, f32[1,1]{1,0:T(1,128)}, f32[1,1]{1,0:T(1,128)}, /*index=5*/f32[1,1]{1,0:T...) fusion(f32[3,4]{1,0:T(4,128)} %param.7), kind=kLoop, calls=%fused_computation.258 | loop fusion | bytes 96 | tf_op jit(solution)/shard_map/slice | solution.py:48
  6.2 1.2 copy.85
  7.5 0.6 and_reduce_fusion.10
  8.4 0.7 broadcast_add_fusion.1
  9.5 1.4 %add_bitcast_fusion.1 = (f32[1,4,128,128]{3,2,1,0:T(8,128)S(1)}, f32[1,4,128,128]{3,2,1,0:T(8,128)S(1)}) fusion(f32[4,128,128]{2,1,0:T(8,128)S(1)} %copy-done, f32[128]{0:T(128)S(1)} %get-tuple-element.36, f32[2,4,128,128]{3,2,1,0:T(8,128)S(1)} %copy-done.1, s32[128]{0:T(128)S(1)} %and_reduce_fusion.8, s32[4,128]{1,0:T(4,128)S(1)} %broadcast_add_fusion), kind=kLoop, calls=%fused_computation.80 | loop fusion | flops 3014656 | bytes 1313792 | tf_op jit(solution)/shard_map/stack | solution.py:65
  10.8 0.8 fusion
  11.6 1.2 convolution_bitcast_fusion.2
  12.9 0.8 fusion.18
  14.0 1.1 pad_maximum_fusion
  15.1 15.0 %all-to-all-start = ((f32[128,16,128]{2,1,0:T(8,128)}), f32[128,16,128]{2,1,0:T(8,128)S(1)}, u32[]{:S(2)}, u32[]{:S(2)}) async-start(f32[128,16,128]{2,1,0:T(8,128)} %pad_maximum_fusion), calls=%async_computation | async-start | bytes 2097152 | tf_op jit(solution)/shard_map/all_to_all | solution.py:40
  39.2 0.5 reshape.414
  39.8 0.5 reshape.415
  40.3 21.2 %all-to-all-done = f32[128,16,128]{2,1,0:T(8,128)S(1)} async-done(((f32[128,16,128]{2,1,0:T(8,128)}), f32[128,16,128]{2,1,0:T(8,128)S(1)}, u32[]{:S(2)}, u32[]{:S(2)}) %all-to-all-start) | async-done | bytes 1048608 | tf_op jit(solution)/shard_map/all_to_all | solution.py:40
  61.6 0.6 fusion.54
  62.3 1.0 add_bitcast_fusion
  63.4 0.6 fusion.4
  63.9 1.3 %convolution_bitcast_fusion.1 = f32[128,2,4,128]{3,2,1,0:T(4,128)S(1)} fusion(f32[128,2,4,128]{3,0,2,1:T(8,128)S(1)} %fusion.4, s32[4,4]{1,0:T(4,128)S(1)} %get-tuple-element.38, f32[]{:T(128)} %bitcast.9, f32[]{:T(128)} %bitcast.8, s32[4,4]{1,0:T(4,128)S(1)} %get-tuple-element.39), kind=kOutput, calls=%fused_computation.1 | convolution fusion | flops 6291744 | bytes 1048712 | tf_op jit(solution)/shard_map/ab,qcbl->qcal/dot_general | solution.py:85
  65.3 0.8 fusion.15
  66.0 1.0 copy.38
  67.0 6.4 %all-to-all-start.1 = ((f32[128,8,128]{2,1,0:T(8,128)}), f32[128,8,128]{2,1,0:T(8,128)S(1)}, u32[]{:S(2)}, u32[]{:S(2)}) async-start(f32[128,8,128]{2,1,0:T(8,128)} %copy.38), calls=%async_computation.1 | async-start | bytes 1048576 | tf_op jit(solution)/shard_map/all_to_all | solution.py:40
  76.8 0.6 constant_dynamic-slice_fusion
  77.5 15.2 %all-to-all-done.1 = f32[128,8,128]{2,1,0:T(8,128)S(1)} async-done(((f32[128,8,128]{2,1,0:T(8,128)}), f32[128,8,128]{2,1,0:T(8,128)S(1)}, u32[]{:S(2)}, u32[]{:S(2)}) %all-to-all-start.1) | async-done | bytes 524320 | tf_op jit(solution)/shard_map/all_to_all | solution.py:40
  92.9 0.8 fusion.42
  93.6 1.6 %fusion.31 = (f32[128,1,4,128]{3,0,2,1:T(8,128)S(1)}, f32[128,1,4,128]{3,0,2,1:T(8,128)S(1)}) fusion(f32[128,2,4,128]{3,0,2,1:T(8,128)S(1)} %fusion.42, f32[128,4,128]{0,2,1:T(8,128)S(1)} %copy.58, f32[]{:T(128)} %bitcast.54), kind=kLoop, calls=%fused_computation.68 | loop fusion | flops 458752 | bytes 1310724 | tf_op jit(solution)/shard_map/stack | solution.py:92
  95.2 0.8 fusion.8
  96.0 1.3 %convolution_bitcast_fusion = f32[128,2,4,128]{3,2,1,0:T(4,128)S(1)} fusion(f32[128,2,4,128]{3,0,2,1:T(8,128)S(1)} %fusion.8, s32[4,4]{1,0:T(4,128)S(1)} %get-tuple-element.38, f32[]{:T(128)} %bitcast.61, f32[]{:T(128)} %bitcast.60, s32[4,4]{1,0:T(4,128)S(1)} %get-tuple-element.39), kind=kOutput, calls=%fused_computation | convolution fusion | flops 6291744 | bytes 1048712 | tf_op jit(solution)/shard_map/ab,rcbq->rcaq/dot_general | solution.py:94
  97.3 0.6 fusion.12
  97.9 1.0 copy.43
  98.9 6.4 %all-to-all-start.2 = ((f32[128,8,128]{2,1,0:T(8,128)}), f32[128,8,128]{2,1,0:T(8,128)S(1)}, u32[]{:S(2)}, u32[]{:S(2)}) async-start(f32[128,8,128]{2,1,0:T(8,128)} %copy.43), calls=%async_computation.2 | async-start | bytes 1048576 | tf_op jit(solution)/shard_map/all_to_all | solution.py:40
  106.8 17.2 %all-to-all-done.2 = f32[128,8,128]{2,1,0:T(8,128)S(1)} async-done(((f32[128,8,128]{2,1,0:T(8,128)}), f32[128,8,128]{2,1,0:T(8,128)S(1)}, u32[]{:S(2)}, u32[]{:S(2)}) %all-to-all-start.2) | async-done | bytes 524320 | tf_op jit(solution)/shard_map/all_to_all | solution.py:40
  124.2 0.8 fusion.51
  125.3 0.8 copy-done.3
  (47 shorter events, 3.7 us)
Async XLA Ops:
  6.1 1.2 copy-start
  7.4 2.1 %copy-start.1 = (f32[2,4,128,128]{3,2,1,0:T(8,128)S(1)}, f32[2,4,128,128]{3,2,1,0:T(8,128)}, u32[]{:S(2)}) copy-start(f32[2,4,128,128]{3,2,1,0:T(8,128)} %param.4) | copy-start | bytes 1572868
  7.5 0.7 copy-start.2
  15.1 46.4 %all-to-all-start = ((f32[128,16,128]{2,1,0:T(8,128)}), f32[128,16,128]{2,1,0:T(8,128)S(1)}, u32[]{:S(2)}, u32[]{:S(2)}) async-start(f32[128,16,128]{2,1,0:T(8,128)} %pad_maximum_fusion), calls=%async_computation | async-start | bytes 2097152 | tf_op jit(solution)/shard_map/all_to_all | solution.py:40
  67.0 25.7 %all-to-all-start.1 = ((f32[128,8,128]{2,1,0:T(8,128)}), f32[128,8,128]{2,1,0:T(8,128)S(1)}, u32[]{:S(2)}, u32[]{:S(2)}) async-start(f32[128,8,128]{2,1,0:T(8,128)} %copy.38), calls=%async_computation.1 | async-start | bytes 1048576 | tf_op jit(solution)/shard_map/all_to_all | solution.py:40
  98.9 25.1 %all-to-all-start.2 = ((f32[128,8,128]{2,1,0:T(8,128)}), f32[128,8,128]{2,1,0:T(8,128)S(1)}, u32[]{:S(2)}, u32[]{:S(2)}) async-start(f32[128,8,128]{2,1,0:T(8,128)} %copy.43), calls=%async_computation.2 | async-start | bytes 1048576 | tf_op jit(solution)/shard_map/all_to_all | solution.py:40
  125.3 0.8 copy-start.3

commit v2 on v0

v2 whole, which is shorter than its diff:
```python
import jax
import jax.numpy as jnp
from jax import lax
from jax.experimental import pallas as pl
from jax.experimental.pallas import tpu as pltpu
from jax.sharding import PartitionSpec as P

SIDE = 128
BITS = 7
BLOCKS = 4
PARTS = 2
TILE = PARTS * BLOCKS
TABLES = 2 * BLOCKS
QB_BITS = 3


def sin_cos(angle, turns=None):
    near = jnp.floor(angle * 0.6366197723675814 + 0.5)
    left = ((angle - near * 1.5703125) - near * 4.837512969970703e-4) - near * 7.549789954891882e-8
    quarter = near.astype(jnp.int32)
    if turns is not None:
        quarter = quarter + turns
    sq = left * left
    sine = left + left * sq * (-1.6666654611e-1 + sq * (8.3321608736e-3 - sq * 1.9515295891e-4))
    cosine = (1.0 - 0.5 * sq) + sq * sq * (
        4.166664568298827e-2 + sq * (-1.388731625493765e-3 + sq * 2.443315711809948e-5)
    )
    odd = (quarter & 1) == 1
    new_sine = jnp.where(odd, cosine, sine)
    new_cosine = jnp.where(odd, sine, cosine)
    new_sine = jnp.where((quarter & 2) != 0, -new_sine, new_sine)
    new_cosine = jnp.where(((quarter + 1) & 2) != 0, -new_cosine, new_cosine)
    return new_sine, new_cosine


def pair_of(angles, layer, group):
    return sin_cos(jnp.full((1, SIDE), angles[layer, group], jnp.float32))


def butterfly(values, pairs):
    values = list(values)
    for bit, (sine, cosine) in enumerate(pairs):
        step = 1 << bit
        for low in range(len(values)):
            if not low & step:
                u, v = values[low], values[low + step]
                values[low] = cosine * u + sine * v
                values[low + step] = cosine * v - sine * u
    return values


def mix_tiles(load, store, pairs):
    for high in range(0, SIDE, 8):
        for i, value in enumerate(butterfly([load(high + i) for i in range(8)], pairs[:3])):
            store(high + i, value, 0)
    for low in range(8):
        order = range(low, SIDE, 8)
        for i, value in zip(order, butterfly([store(i, None, 0) for i in order], pairs[3:])):
            store(i, value, 1)


def weights(pairs):
    lane = lax.broadcasted_iota(jnp.int32, (8, SIDE), 1)
    sub = lax.broadcasted_iota(jnp.int32, (8, SIDE), 0)

    def factor(bit, of):
        to = (lane >> bit) & 1
        sine, cosine = pairs[bit]
        return jnp.where(of == to, cosine, jnp.where(to == 1, -sine, sine))

    matrix = factor(0, sub & 1) * factor(1, (sub >> 1) & 1) * factor(2, (sub >> 2) & 1)
    for bit in range(3, BITS):
        ends = [factor(bit, jnp.full((8, SIDE), of, jnp.int32)) for of in (0, 1)]
        pieces = matrix.shape[0] // 8
        matrix = jnp.concatenate(
            [matrix[8 * i : 8 * i + 8] * end for end in ends for i in range(pieces)], axis=0
        )
    high = matrix.astype(jnp.bfloat16)
    low = (matrix - high.astype(jnp.float32)).astype(jnp.bfloat16)
    both = jnp.concatenate([high, low], axis=1)
    return jnp.concatenate([both, both], axis=0)


def mix_lanes(values, both):
    high = values.astype(jnp.bfloat16)
    low = (values - high.astype(jnp.float32)).astype(jnp.bfloat16)
    out = jnp.dot(
        jnp.concatenate([high, low], axis=1), both, preferred_element_type=jnp.float32
    )
    return out[:, :SIDE] + out[:, SIDE:]


def bit_counts(place):
    row = lax.broadcasted_iota(jnp.int32, (SIDE, SIDE), 0)
    lane = lax.broadcasted_iota(jnp.int32, (SIDE, SIDE), 1)
    total = jnp.full((SIDE, SIDE), place, jnp.int32)
    count = jnp.zeros((SIDE, SIDE), jnp.int32)
    for bit in range(BITS):
        count = count + ((row >> bit) & 1) + ((lane >> bit) & 1) + ((total >> bit) & 1)
    return count


def every(step, first, count=SIDE):
    return pl.ds(first, count, stride=step)


def turned(real, imag, sine, cosine):
    return real * cosine + imag * sine, imag * cosine - real * sine


def mix_blocks(parts, pair):
    return [butterfly(part, [pair] * 2) for part in parts]


def in_buffer(buffer, out=None, step=TILE):
    def store(index, value, last):
        if value is None:
            return buffer[TILE * index : TILE * index + TILE, :]
        if last and out is not None:
            out[step * index : step * index + TILE, :] = value
        else:
            buffer[TILE * index : TILE * index + TILE, :] = value

    return store


def first_kernel(angles, place, diagonal, wave, levels, out, buffer):
    group = [pair_of(angles, 0, g) for g in range(4)]
    lane_mix = weights([group[0]] * BITS)
    count = bit_counts(place[0, 0])
    speed = diagonal[0:1, :]
    real, imag = [], []
    for b in range(BLOCKS):
        level = levels[b]
        sine, cosine = sin_cos(level * speed, count + b.bit_count())
        r, i = turned(wave[0, b], wave[1, b], sine, cosine)
        real.append(r)
        imag.append(i)
        out[every(TILE + TABLES, TILE + b), :] = level
        out[every(TILE + TABLES, TILE + BLOCKS + b), :] = level.T
    for p, part in enumerate(mix_blocks((real, imag), group[2])):
        for b in range(BLOCKS):
            buffer[every(TILE, p * BLOCKS + b), :] = mix_lanes(part[b], lane_mix)
    store = in_buffer(buffer, out, TILE + TABLES)
    mix_tiles(lambda i: store(i, None, 0), store, [group[1]] * BITS)


def second_kernel(angles, diagonal, got, out, turned_levels, buffer):
    q_pairs = [pair_of(angles, 0, 3)] * QB_BITS + [pair_of(angles, 0, 2)] * (BITS - QB_BITS)
    step = TILE + TABLES
    store = in_buffer(buffer)
    mix_tiles(lambda i: got[step * i : step * i + TILE, :], store, q_pairs)
    group = [pair_of(angles, 1, g) for g in range(4)]
    lane_mix = weights([group[0]] * BITS)
    q_mix = weights([group[3]] * QB_BITS + [group[2]] * (BITS - QB_BITS))
    speed = diagonal[1:2, :]
    real, imag = [], []
    for b in range(BLOCKS):
        sine, cosine = sin_cos(got[every(step, TILE + b), :] * speed)
        r, i = turned(
            buffer[every(TILE, b), :], buffer[every(TILE, BLOCKS + b), :], sine, cosine
        )
        real.append(r)
        imag.append(i)
        turned_levels[b] = got[every(step, TILE + BLOCKS + b), :].T
    for p, part in enumerate(mix_blocks((real, imag), group[2])):
        for b in range(BLOCKS):
            out[every(TILE, p * BLOCKS + b), :] = mix_lanes(mix_lanes(part[b], lane_mix).T, q_mix)


def third_kernel(angles, place, diagonal, got, turned_levels, out, buffer):
    store = in_buffer(buffer)
    mix_tiles(
        lambda i: got[TILE * i : TILE * i + TILE, :], store, [pair_of(angles, 1, 1)] * BITS
    )
    group = [pair_of(angles, 2, g) for g in range(4)]
    q_mix = weights([group[3]] * QB_BITS + [group[2]] * (BITS - QB_BITS))
    row_mix = weights([group[1]] * BITS)
    lane = lax.broadcasted_iota(jnp.int32, (1, SIDE), 1)
    speed = jnp.sum(jnp.where(lane == place[0, 0], diagonal[2:3, :], 0.0), axis=1, keepdims=True)
    real, imag = [], []
    for b in range(BLOCKS):
        sine, cosine = sin_cos(turned_levels[b] * speed)
        r, i = turned(
            buffer[every(TILE, b), :], buffer[every(TILE, BLOCKS + b), :], sine, cosine
        )
        real.append(r)
        imag.append(i)
    for p, part in enumerate(mix_blocks((real, imag), group[2])):
        for b in range(BLOCKS):
            out[every(TILE, p * BLOCKS + b), :] = mix_lanes(mix_lanes(part[b], q_mix).T, row_mix)


def last_kernel(angles, place, got, out, buffer):
    store = in_buffer(buffer)
    mix_tiles(
        lambda i: got[TILE * i : TILE * i + TILE, :], store, [pair_of(angles, 2, 0)] * BITS
    )
    count = bit_counts(place[0, 0])
    for b in range(BLOCKS):
        real, imag = (buffer[every(TILE, p * BLOCKS + b), :].T for p in range(PARTS))
        turns = count + b.bit_count()
        odd = (turns & 1) == 1
        new_real, new_imag = jnp.where(odd, -imag, real), jnp.where(odd, real, imag)
        back = (turns & 2) != 0
        out[0, b] = jnp.where(back, -new_real, new_real)
        out[1, b] = jnp.where(back, -new_imag, new_imag)


def call(kernel, name, operands, outs, interpret=False):
    small = pl.BlockSpec(memory_space=pltpu.SMEM)
    big = pl.BlockSpec(memory_space=pltpu.VMEM)
    specs = [small if o.size <= 16 else big for o in operands]
    shapes = [jax.ShapeDtypeStruct(s, jnp.float32) for s in outs]
    return pl.pallas_call(
        kernel,
        name=name,
        in_specs=specs,
        out_specs=[big] * len(outs),
        out_shape=shapes,
        scratch_shapes=[pltpu.VMEM((SIDE * TILE, SIDE), jnp.float32)],
        compiler_params=pltpu.CompilerParams(vmem_limit_bytes=32 * 1024 * 1024),
        interpret=interpret,
    )(*operands)


def exchange(values):
    shape = values.shape
    moved = lax.all_to_all(
        values.reshape(SIDE, -1, SIDE), ("qa", "qb"), split_axis=0, concat_axis=0, tiled=True
    )
    return moved.reshape(shape)


def stages(interpret=False):
    tile = (SIDE * TILE, SIDE)

    def first(angles, place, diagonal, wave, levels):
        shape = (SIDE * (TILE + TABLES), SIDE)
        return call(first_kernel, "first", (angles, place, diagonal, wave, levels), [shape], interpret)[0]

    def second(angles, diagonal, got):
        return call(
            second_kernel, "second", (angles, diagonal, got), [tile, (BLOCKS, SIDE, SIDE)], interpret
        )

    def third(angles, place, diagonal, got, levels):
        return call(third_kernel, "third", (angles, place, diagonal, got, levels), [tile], interpret)[0]

    def last(angles, place, got):
        return call(
            last_kernel, "last", (angles, place, got), [(PARTS, BLOCKS, SIDE, SIDE)], interpret
        )[0]

    return first, second, third, last


def shards(wave_parts, level_table, diagonal_angles, turn_angles):
    place = lax.axis_index("qa") * lax.axis_size("qb") + lax.axis_index("qb")
    place = jnp.full((1, 1), place, jnp.int32)
    first, second, third, last = stages()
    got = exchange(first(turn_angles, place, diagonal_angles, wave_parts, level_table))
    values, levels = second(turn_angles, diagonal_angles, got)
    values = third(turn_angles, place, diagonal_angles, exchange(values), levels)
    return last(turn_angles, place, exchange(values))


def solution(mesh):
    placed = (
        P("trial", ("qa", "qb"), None, None),
        P(("trial", "qa", "qb"), None, None),
        P("trial", None),
        P("trial", None),
    )
    return jax.shard_map(
        shards,
        mesh=mesh,
        in_specs=placed,
        out_specs=P("trial", ("qa", "qb"), None, None),
        check_vma=False,
    )
```

time: 246 us -> 107 us (0.43)
  waiting for transfers between devices: 84 us -> 0 us
  starting transfers between devices: 46 us -> 0 us
  blocking collectives: 55.1 us -> 95.7 us
  matrix products: 20.9 us -> 0 us
  between operations: 17.6 us -> 0.02 us
  local copies, waits for them, and re-layouts: 15.4 us -> 2.69 us
  Pallas kernels: 0 us -> 7.95 us
  other arithmetic: 5.26 us -> 0 us
    all_to_all x8 -> x0, waiting for transfers between devices: 84 us -> none  [the longest x3 35.8 us: shards(): lax.all_to_all(values, 'qb', split_axis=3, concat_axis=1, tiled=True)]
    all_to_all x8 -> x0, starting transfers between devices: 46 us -> none  [the longest x3 18.5 us: shards(): lax.all_to_all(values, 'qb', split_axis=3, concat_axis=1, tiled=True)]
    all_to_all x4 -> x3, blocking collectives: 55.1 us -> 95.7 us  [exchange(): lax.all_to_all(values.reshape(SIDE, -1, SIDE), ('qa', 'qb'), split_axis=0...]
    dot_general x24 -> x0, matrix products: 20.9 us -> none  [times(): jnp.tensordot(values, table, axes=([dim], [0]), precision=lax.Precision.H...]
    pallas_call x0 -> x4, Pallas kernels: none -> 7.95 us  [call(): pl.pallas_call(kernel, name=name, in_specs=specs, out_specs=[big] * len(o...]
    another operation x9 -> x0, local copies, waits for them, and re-layouts: 5.69 us -> none  [mix_dim(): return jnp.stack([by_real[0] - by_imag[1], by_real[1] + by_imag[0]])]
    all_to_all x16 -> x0, local copies, waits for them, and re-layouts: 5.52 us -> none  [the longest x6 3.09 us: shards(): lax.all_to_all(moved, 'qa', split_axis=1, concat_axis=2, tiled=True)]
    another operation x12 -> x0, other arithmetic: 4.42 us -> none  [the longest x3 4.08 us: phase_step(): jnp.stack([values[0] * jnp.cos(turn) + values[1] * jnp.sin(turn), values[...]
  transfers between devices with their start and end apart: 8 -> 0, of which waited for: 8 -> 0; matrix products, arithmetic and copies ran while one was open for 0% -> 0% of each run, Pallas kernels for 0% -> 0%
where the time goes in v2:
time: 107 us; the launch traced here: 106 us
  blocking collectives  95.7 us (89%)
  Pallas kernels  7.95 us (7%)
  local copies, waits for them, and re-layouts  2.69 us (3%)
    all_to_all x3, blocking collectives, exchange(): lax.all_to_all(values.reshape(SIDE, -1, SIDE), ('qa', 'qb'), split_axis=0...  95.7 us
    pallas_call x4, Pallas kernels, call(): pl.pallas_call(kernel, name=name, in_specs=specs, out_specs=[big] * len(o...  7.95 us
    unnamed x8, local copies, waits for them, and re-layouts  2.69 us

profile of v2, /device:TPU:32, one launch (start us, length us, event | category | flops | bytes accessed | tf_op | source)
XLA Modules:
  0.0 106.4 jit_solution(16221485790493902492)
XLA Ops:
  0.0 0.0 copy-start.3
  0.0 0.0 copy-start.2
  0.0 0.7 copy-done.3
  0.7 0.0 copy-done.2
  0.7 0.0 copy-start
  0.7 1.0 copy-done
  1.7 0.0 copy-start.1
  1.7 0.9 copy-done.1
  2.7 1.9 %first.1 = f32[2048,128]{1,0:T(8,128)S(1)} custom-call(f32[3,4]{1,0:T(4,128)S(1)} %copy-done.2, s32[1,1]{1,0:T(1,128)} %bitcast.place, f32[3,128]{1,0:T(4,128)S(1)} %copy-done.3, f32[2,4,128,128]{3,2,1,0:T(8,128)S(1)} %copy-done, f32[4,128,128]{2,1,0:T(8,128)S(1)} %copy-done.1), custom_call_target="tpu_custom_call" | custom-call | tf_op jit(solution)/shard_map/first/pallas_call | solution.py:215
  4.6 45.9 %all_to_all.15 = f32[128,16,128]{2,1,0:T(8,128)S(1)} all-to-all(f32[128,16,128]{2,1,0:T(8,128)S(1)} %bitcast.8), channel_id=1, replica_groups=mesh['trial'=2,'qa'=16,'qb'=8] {'qa','qb'}, dimensions={0} | all-to-all | bytes 2097152 | tf_op jit(solution)/shard_map/all_to_all | solution.py:229
  50.5 2.0 %second.1 = (f32[1024,128]{1,0:T(8,128)S(1)}, f32[4,128,128]{2,1,0:T(8,128)S(1)}) custom-call(f32[3,4]{1,0:T(4,128)S(1)} %copy-done.2, f32[3,128]{1,0:T(4,128)S(1)} %copy-done.3, f32[2048,128]{1,0:T(8,128)S(1)} %bitcast.7), custom_call_target="tpu_custom_call" | custom-call | tf_op jit(solution)/shard_map/second/pallas_call | solution.py:215
  52.6 25.3 %all_to_all.16 = f32[128,8,128]{2,1,0:T(8,128)S(1)} all-to-all(f32[128,8,128]{2,1,0:T(8,128)S(1)} %bitcast.12), channel_id=1, replica_groups=mesh['trial'=2,'qa'=16,'qb'=8] {'qa','qb'}, dimensions={0} | all-to-all | bytes 1048576 | tf_op jit(solution)/shard_map/all_to_all | solution.py:229
  77.9 2.0 %third.1 = f32[1024,128]{1,0:T(8,128)S(1)} custom-call(f32[3,4]{1,0:T(4,128)S(1)} %copy-done.2, s32[1,1]{1,0:T(1,128)} %bitcast.place, f32[3,128]{1,0:T(4,128)S(1)} %copy-done.3, f32[1024,128]{1,0:T(8,128)S(1)} %bitcast.9, f32[4,128,128]{2,1,0:T(8,128)S(1)} %get-tuple-element.8.turned_levels), custom_call_target="tpu_custom_call" | custom-call | tf_op jit(solution)/shard_map/third/pallas_call | solution.py:215
  79.9 24.4 %all_to_all.17 = f32[128,8,128]{2,1,0:T(8,128)S(1)} all-to-all(f32[128,8,128]{2,1,0:T(8,128)S(1)} %bitcast.10), channel_id=1, replica_groups=mesh['trial'=2,'qa'=16,'qb'=8] {'qa','qb'}, dimensions={0} | all-to-all | bytes 1048576 | tf_op jit(solution)/shard_map/all_to_all | solution.py:229
  104.4 2.0 %last.1 = f32[2,4,128,128]{3,2,1,0:T(8,128)} custom-call(f32[3,4]{1,0:T(4,128)S(1)} %copy-done.2, s32[1,1]{1,0:T(1,128)} %bitcast.place, f32[1024,128]{1,0:T(8,128)S(1)} %bitcast.11), custom_call_target="tpu_custom_call" | custom-call | tf_op jit(solution)/shard_map/last/pallas_call | solution.py:215
Async XLA Ops:
  0.0 0.7 copy-start.3
  0.0 0.7 copy-start.2
  0.7 1.0 copy-start
  1.7 0.9 copy-start.1

commit v3 on v2

--- a/solution.py
+++ b/solution.py
@@ -10,7 +10,7 @@
 BLOCKS = 4
 PARTS = 2
 TILE = PARTS * BLOCKS
-TABLES = 2 * BLOCKS
+WIDE = TILE + BLOCKS
 QB_BITS = 3
 
 
@@ -34,7 +34,7 @@
 
 
 def pair_of(angles, layer, group):
-    return sin_cos(jnp.full((1, SIDE), angles[layer, group], jnp.float32))
+    return sin_cos(jnp.broadcast_to(angles[layer : layer + 1, group : group + 1], (1, SIDE)))
 
 
 def butterfly(values, pairs):
@@ -90,6 +90,10 @@
     return out[:, :SIDE] + out[:, SIDE:]
 
 
+def own_place():
+    return lax.axis_index("qa") * lax.axis_size("qb") + lax.axis_index("qb")
+
+
 def bit_counts(place):
     row = lax.broadcasted_iota(jnp.int32, (SIDE, SIDE), 0)
     lane = lax.broadcasted_iota(jnp.int32, (SIDE, SIDE), 1)
@@ -124,10 +128,10 @@
     return store
 
 
-def first_kernel(angles, place, diagonal, wave, levels, out, buffer):
+def first_kernel(angles, diagonal, wave, levels, out, buffer):
     group = [pair_of(angles, 0, g) for g in range(4)]
     lane_mix = weights([group[0]] * BITS)
-    count = bit_counts(place[0, 0])
+    count = bit_counts(own_place())
     speed = diagonal[0:1, :]
     real, imag = [], []
     for b in range(BLOCKS):
@@ -136,67 +140,65 @@
         r, i = turned(wave[0, b], wave[1, b], sine, cosine)
         real.append(r)
         imag.append(i)
-        out[every(TILE + TABLES, TILE + b), :] = level
-        out[every(TILE + TABLES, TILE + BLOCKS + b), :] = level.T
+        out[every(WIDE, TILE + b), :] = level
     for p, part in enumerate(mix_blocks((real, imag), group[2])):
         for b in range(BLOCKS):
             buffer[every(TILE, p * BLOCKS + b), :] = mix_lanes(part[b], lane_mix)
-    store = in_buffer(buffer, out, TILE + TABLES)
+    store = in_buffer(buffer, out, WIDE)
     mix_tiles(lambda i: store(i, None, 0), store, [group[1]] * BITS)
 
 
-def second_kernel(angles, diagonal, got, out, turned_levels, buffer):
-    q_pairs = [pair_of(angles, 0, 3)] * QB_BITS + [pair_of(angles, 0, 2)] * (BITS - QB_BITS)
-    step = TILE + TABLES
+def middle(layer, got, out, buffer, before, speed, lane_mix, next_mix, group, send_levels):
     store = in_buffer(buffer)
-    mix_tiles(lambda i: got[step * i : step * i + TILE, :], store, q_pairs)
-    group = [pair_of(angles, 1, g) for g in range(4)]
-    lane_mix = weights([group[0]] * BITS)
-    q_mix = weights([group[3]] * QB_BITS + [group[2]] * (BITS - QB_BITS))
-    speed = diagonal[1:2, :]
+    mix_tiles(lambda i: got[WIDE * i : WIDE * i + TILE, :], store, before)
+    step = WIDE if send_levels else TILE
     real, imag = [], []
     for b in range(BLOCKS):
-        sine, cosine = sin_cos(got[every(step, TILE + b), :] * speed)
+        level = got[every(WIDE, TILE + b), :]
+        sine, cosine = sin_cos(level * speed)
         r, i = turned(
             buffer[every(TILE, b), :], buffer[every(TILE, BLOCKS + b), :], sine, cosine
         )
         real.append(r)
         imag.append(i)
-        turned_levels[b] = got[every(step, TILE + BLOCKS + b), :].T
+        if send_levels:
+            out[every(step, TILE + b), :] = level.T
     for p, part in enumerate(mix_blocks((real, imag), group[2])):
         for b in range(BLOCKS):
-            out[every(TILE, p * BLOCKS + b), :] = mix_lanes(mix_lanes(part[b], lane_mix).T, q_mix)
-
-
-def third_kernel(angles, place, diagonal, got, turned_levels, out, buffer):
-    store = in_buffer(buffer)
-    mix_tiles(
-        lambda i: got[TILE * i : TILE * i + TILE, :], store, [pair_of(angles, 1, 1)] * BITS
-    )
+            mixed = mix_lanes(mix_lanes(part[b], lane_mix).T, next_mix)
+            out[every(step, p * BLOCKS + b), :] = mixed
+
+
+def q_pairs(qa_pair, qb_pair):
+    return [qb_pair] * QB_BITS + [qa_pair] * (BITS - QB_BITS)
+
+
+def second_kernel(angles, diagonal, got, out, buffer):
+    before = q_pairs(pair_of(angles, 0, 2), pair_of(angles, 0, 3))
+    group = [pair_of(angles, 1, g) for g in range(4)]
+    lane_mix = weights([group[0]] * BITS)
+    q_mix = weights(q_pairs(group[2], group[3]))
+    middle(1, got, out, buffer, before, diagonal[1:2, :], lane_mix, q_mix, group, True)
+
+
+def third_kernel(angles, diagonal, got, out, buffer):
     group = [pair_of(angles, 2, g) for g in range(4)]
-    q_mix = weights([group[3]] * QB_BITS + [group[2]] * (BITS - QB_BITS))
+    q_mix = weights(q_pairs(group[2], group[3]))
     row_mix = weights([group[1]] * BITS)
     lane = lax.broadcasted_iota(jnp.int32, (1, SIDE), 1)
-    speed = jnp.sum(jnp.where(lane == place[0, 0], diagonal[2:3, :], 0.0), axis=1, keepdims=True)
-    real, imag = [], []
-    for b in range(BLOCKS):
-        sine, cosine = sin_cos(turned_levels[b] * speed)
-        r, i = turned(
-            buffer[every(TILE, b), :], buffer[every(TILE, BLOCKS + b), :], sine, cosine
-        )
-        real.append(r)
-        imag.append(i)
-    for p, part in enumerate(mix_blocks((real, imag), group[2])):
-        for b in range(BLOCKS):
-            out[every(TILE, p * BLOCKS + b), :] = mix_lanes(mix_lanes(part[b], q_mix).T, row_mix)
-
-
-def last_kernel(angles, place, got, out, buffer):
+    own = jnp.where(lane == own_place(), diagonal[2:3, :], 0.0)
+    speed = jnp.sum(own, axis=1, keepdims=True)
+    before = [pair_of(angles, 1, 1)] * BITS
+    middle(2, got, out, buffer, before, speed, q_mix, row_mix, group, False)
+
+
+def last_kernel(angles, got, out_far, buffer, out, sems):
     store = in_buffer(buffer)
     mix_tiles(
         lambda i: got[TILE * i : TILE * i + TILE, :], store, [pair_of(angles, 2, 0)] * BITS
     )
-    count = bit_counts(place[0, 0])
+    count = bit_counts(own_place())
+    copies = []
     for b in range(BLOCKS):
         real, imag = (buffer[every(TILE, p * BLOCKS + b), :].T for p in range(PARTS))
         turns = count + b.bit_count()
@@ -205,64 +207,65 @@
         back = (turns & 2) != 0
         out[0, b] = jnp.where(back, -new_real, new_real)
         out[1, b] = jnp.where(back, -new_imag, new_imag)
-
-
-def call(kernel, name, operands, outs, interpret=False):
-    small = pl.BlockSpec(memory_space=pltpu.SMEM)
-    big = pl.BlockSpec(memory_space=pltpu.VMEM)
-    specs = [small if o.size <= 16 else big for o in operands]
-    shapes = [jax.ShapeDtypeStruct(s, jnp.float32) for s in outs]
+        for p in range(PARTS):
+            copy = pltpu.make_async_copy(out.at[p, b], out_far.at[p, b], sems.at[p, b])
+            copy.start()
+            copies.append(copy)
+    for copy in copies:
+        copy.wait()
+
+
+NEAR = pl.BlockSpec(memory_space=pltpu.VMEM)
+FAR = pl.BlockSpec(memory_space=pl.ANY)
+STATE = (PARTS, BLOCKS, SIDE, SIDE)
+
+
+def call(kernel, name, operands, in_specs, out_shape, out_spec=NEAR, scratch=()):
     return pl.pallas_call(
         kernel,
         name=name,
-        in_specs=specs,
-        out_specs=[big] * len(outs),
-        out_shape=shapes,
-        scratch_shapes=[pltpu.VMEM((SIDE * TILE, SIDE), jnp.float32)],
+        in_specs=in_specs,
+        out_specs=out_spec,
+        out_shape=jax.ShapeDtypeStruct(out_shape, jnp.float32),
+        scratch_shapes=[pltpu.VMEM((SIDE * TILE, SIDE), jnp.float32), *scratch],
         compiler_params=pltpu.CompilerParams(vmem_limit_bytes=32 * 1024 * 1024),
-        interpret=interpret,
+        interpret=INTERPRET,
     )(*operands)
 
 
+INTERPRET = False
+
+
 def exchange(values):
-    shape = values.shape
+    rows = values.shape[0] // SIDE
+    shape = (SIDE, rows // 8, 8, SIDE) if rows % 8 == 0 else (SIDE, rows // 4, 4, SIDE)
     moved = lax.all_to_all(
-        values.reshape(SIDE, -1, SIDE), ("qa", "qb"), split_axis=0, concat_axis=0, tiled=True
-    )
-    return moved.reshape(shape)
-
-
-def stages(interpret=False):
-    tile = (SIDE * TILE, SIDE)
-
-    def first(angles, place, diagonal, wave, levels):
-        shape = (SIDE * (TILE + TABLES), SIDE)
-        return call(first_kernel, "first", (angles, place, diagonal, wave, levels), [shape], interpret)[0]
-
-    def second(angles, diagonal, got):
-        return call(
-            second_kernel, "second", (angles, diagonal, got), [tile, (BLOCKS, SIDE, SIDE)], interpret
-        )
-
-    def third(angles, place, diagonal, got, levels):
-        return call(third_kernel, "third", (angles, place, diagonal, got, levels), [tile], interpret)[0]
-
-    def last(angles, place, got):
-        return call(
-            last_kernel, "last", (angles, place, got), [(PARTS, BLOCKS, SIDE, SIDE)], interpret
-        )[0]
-
-    return first, second, third, last
+        values.reshape(shape), ("qa", "qb"), split_axis=0, concat_axis=0, tiled=True
+    )
+    return moved.reshape(values.shape)
 
 
 def shards(wave_parts, level_table, diagonal_angles, turn_angles):
-    place = lax.axis_index("qa") * lax.axis_size("qb") + lax.axis_index("qb")
-    place = jnp.full((1, 1), place, jnp.int32)
-    first, second, third, last = stages()
-    got = exchange(first(turn_angles, place, diagonal_angles, wave_parts, level_table))
-    values, levels = second(turn_angles, diagonal_angles, got)
-    values = third(turn_angles, place, diagonal_angles, exchange(values), levels)
-    return last(turn_angles, place, exchange(values))
+    wide, narrow = (SIDE * WIDE, SIDE), (SIDE * TILE, SIDE)
+    small = (turn_angles, diagonal_angles)
+    values = call(
+        first_kernel,
+        "first",
+        (*small, wave_parts, level_table),
+        [NEAR] * 4,
+        wide,
+    )
+    values = call(second_kernel, "second", (*small, exchange(values)), [NEAR] * 3, wide)
+    values = call(third_kernel, "third", (*small, exchange(values)), [NEAR] * 3, narrow)
+    return call(
+        last_kernel,
+        "last",
+        (turn_angles, exchange(values)),
+        [NEAR] * 2,
+        STATE,
+        FAR,
+        scratch=[pltpu.VMEM(STATE, jnp.float32), pltpu.SemaphoreType.DMA((PARTS, BLOCKS))],
+    )
 
 
 def solution(mesh):

time: 107 us -> 105 us (0.981)
  Pallas kernels: 7.95 us -> 5.75 us
    pallas_call x4, Pallas kernels: 7.95 us -> 5.75 us  [call(): pl.pallas_call(kernel, name=name, in_specs=in_specs, out_specs=out_spec,...]
where the time goes in v3:
time: 105 us; the launch traced here: 104 us
  blocking collectives  95.2 us (91%)
  Pallas kernels  5.75 us (5%)
  local copies, waits for them, and re-layouts  3.35 us (3%)
    all_to_all x3, blocking collectives, exchange(): lax.all_to_all(values.reshape(shape), ('qa', 'qb'), split_axis=0, concat_...  95.2 us
    pallas_call x4, Pallas kernels, call(): pl.pallas_call(kernel, name=name, in_specs=in_specs, out_specs=out_spec,...  5.75 us
    unnamed x8, local copies, waits for them, and re-layouts  3.35 us

profile of v3, /device:TPU:32, one launch (start us, length us, event | category | flops | bytes accessed | tf_op | source)
XLA Modules:
  0.0 104.3 jit_solution(897943699172598444)
XLA Ops:
  0.0 0.0 copy-start
  0.0 1.0 copy-done
  1.0 0.0 copy-start.1
  1.0 0.9 copy-done.1
  2.0 0.0 copy-start.2
  2.0 0.7 copy-done.2
  2.7 0.0 copy-start.3
  2.7 0.7 copy-done.3
  3.4 1.3 %first.1 = f32[1536,128]{1,0:T(8,128)S(1)} custom-call(f32[3,4]{1,0:T(4,128)S(1)} %copy-done.2, f32[3,128]{1,0:T(4,128)S(1)} %copy-done.3, f32[2,4,128,128]{3,2,1,0:T(8,128)S(1)} %copy-done, f32[4,128,128]{2,1,0:T(8,128)S(1)} %copy-done.1), custom_call_target="tpu_custom_call" | custom-call | tf_op jit(solution)/shard_map/first/pallas_call | solution.py:224
  4.6 40.5 %all_to_all.15 = f32[128,3,4,128]{3,2,1,0:T(4,128)S(1)} all-to-all(f32[128,3,4,128]{3,2,1,0:T(4,128)S(1)} %bitcast.11), channel_id=1, replica_groups=mesh['trial'=2,'qa'=16,'qb'=8] {'qa','qb'}, dimensions={0} | all-to-all | bytes 1572864 | tf_op jit(solution)/shard_map/all_to_all | solution.py:242
  45.1 1.5 %second.1 = f32[1536,128]{1,0:T(8,128)S(1)} custom-call(f32[3,4]{1,0:T(4,128)S(1)} %copy-done.2, f32[3,128]{1,0:T(4,128)S(1)} %copy-done.3, f32[1536,128]{1,0:T(8,128)S(1)} %bitcast.8), custom_call_target="tpu_custom_call" | custom-call | tf_op jit(solution)/shard_map/second/pallas_call | solution.py:224
  46.6 30.6 %all_to_all.16 = f32[128,3,4,128]{3,2,1,0:T(4,128)S(1)} all-to-all(f32[128,3,4,128]{3,2,1,0:T(4,128)S(1)} %bitcast.9), channel_id=1, replica_groups=mesh['trial'=2,'qa'=16,'qb'=8] {'qa','qb'}, dimensions={0} | all-to-all | bytes 1572864 | tf_op jit(solution)/shard_map/all_to_all | solution.py:242
  77.2 1.5 %third.1 = f32[1024,128]{1,0:T(8,128)S(1)} custom-call(f32[3,4]{1,0:T(4,128)S(1)} %copy-done.2, f32[3,128]{1,0:T(4,128)S(1)} %copy-done.3, f32[1536,128]{1,0:T(8,128)S(1)} %bitcast.10), custom_call_target="tpu_custom_call" | custom-call | tf_op jit(solution)/shard_map/third/pallas_call | solution.py:224
  78.7 24.1 %all_to_all.17 = f32[128,1,8,128]{3,2,1,0:T(8,128)S(1)} all-to-all(f32[128,1,8,128]{3,2,1,0:T(8,128)S(1)} %bitcast.12), channel_id=1, replica_groups=mesh['trial'=2,'qa'=16,'qb'=8] {'qa','qb'}, dimensions={0} | all-to-all | bytes 1048576 | tf_op jit(solution)/shard_map/all_to_all | solution.py:242
  102.8 1.5 %last.1 = f32[2,4,128,128]{3,2,1,0:T(8,128)} custom-call(f32[3,4]{1,0:T(4,128)S(1)} %copy-done.2, f32[1024,128]{1,0:T(8,128)S(1)} %bitcast.13), custom_call_target="tpu_custom_call" | custom-call | tf_op jit(solution)/shard_map/last/pallas_call | solution.py:224
Async XLA Ops:
  0.0 1.0 copy-start
  1.0 0.9 copy-start.1
  2.0 0.7 copy-start.2
  2.7 0.7 copy-start.3

commit v4 on v3

--- a/solution.py
+++ b/solution.py
@@ -6,6 +6,7 @@
 from jax.sharding import PartitionSpec as P
 
 SIDE = 128
+LAYERS = 3
 BITS = 7
 BLOCKS = 4
 PARTS = 2
@@ -16,7 +17,7 @@
 
 def sin_cos(angle, turns=None):
     near = jnp.floor(angle * 0.6366197723675814 + 0.5)
-    left = ((angle - near * 1.5703125) - near * 4.837512969970703e-4) - near * 7.549789954891882e-8
+    left = (angle - near * 1.5703125) - near * 4.8382679489661926e-4
     quarter = near.astype(jnp.int32)
     if turns is not None:
         quarter = quarter + turns
@@ -34,19 +35,28 @@
 
 
 def pair_of(angles, layer, group):
-    return sin_cos(jnp.broadcast_to(angles[layer : layer + 1, group : group + 1], (1, SIDE)))
+    row = LAYERS + layer
+    sine, cosine = sin_cos(jnp.broadcast_to(angles[row : row + 1, group : group + 1], (1, SIDE)))
+    return sine, cosine, sine / cosine
 
 
 def butterfly(values, pairs):
     values = list(values)
-    for bit, (sine, cosine) in enumerate(pairs):
+    for bit, (_, _, tangent) in enumerate(pairs):
         step = 1 << bit
         for low in range(len(values)):
             if not low & step:
                 u, v = values[low], values[low + step]
-                values[low] = cosine * u + sine * v
-                values[low + step] = cosine * v - sine * u
+                values[low] = u + tangent * v
+                values[low + step] = v - tangent * u
     return values
+
+
+def shrink(pairs):
+    product = pairs[0][1]
+    for pair in pairs[1:]:
+        product = product * pair[1]
+    return product
 
 
 def mix_tiles(load, store, pairs):
@@ -59,16 +69,16 @@
             store(i, value, 1)
 
 
-def weights(pairs):
+def weights(pairs, scale=1.0):
     lane = lax.broadcasted_iota(jnp.int32, (8, SIDE), 1)
     sub = lax.broadcasted_iota(jnp.int32, (8, SIDE), 0)
 
     def factor(bit, of):
         to = (lane >> bit) & 1
-        sine, cosine = pairs[bit]
+        sine, cosine, _ = pairs[bit]
         return jnp.where(of == to, cosine, jnp.where(to == 1, -sine, sine))
 
-    matrix = factor(0, sub & 1) * factor(1, (sub >> 1) & 1) * factor(2, (sub >> 2) & 1)
+    matrix = scale * factor(0, sub & 1) * factor(1, (sub >> 1) & 1) * factor(2, (sub >> 2) & 1)
     for bit in range(3, BITS):
         ends = [factor(bit, jnp.full((8, SIDE), of, jnp.int32)) for of in (0, 1)]
         pieces = matrix.shape[0] // 8
@@ -128,11 +138,12 @@
     return store
 
 
-def first_kernel(angles, diagonal, wave, levels, out, buffer):
+def first_kernel(angles, wave, levels, out, buffer):
     group = [pair_of(angles, 0, g) for g in range(4)]
-    lane_mix = weights([group[0]] * BITS)
+    after = [group[1]] * BITS
+    lane_mix = weights([group[0]] * BITS, shrink(after + [group[2]] * 2))
     count = bit_counts(own_place())
-    speed = diagonal[0:1, :]
+    speed = angles[0:1, :]
     real, imag = [], []
     for b in range(BLOCKS):
         level = levels[b]
@@ -145,7 +156,7 @@
         for b in range(BLOCKS):
             buffer[every(TILE, p * BLOCKS + b), :] = mix_lanes(part[b], lane_mix)
     store = in_buffer(buffer, out, WIDE)
-    mix_tiles(lambda i: store(i, None, 0), store, [group[1]] * BITS)
+    mix_tiles(lambda i: store(i, None, 0), store, after)
 
 
 def middle(layer, got, out, buffer, before, speed, lane_mix, next_mix, group, send_levels):
@@ -173,22 +184,22 @@
     return [qb_pair] * QB_BITS + [qa_pair] * (BITS - QB_BITS)
 
 
-def second_kernel(angles, diagonal, got, out, buffer):
+def second_kernel(angles, got, out, buffer):
     before = q_pairs(pair_of(angles, 0, 2), pair_of(angles, 0, 3))
     group = [pair_of(angles, 1, g) for g in range(4)]
-    lane_mix = weights([group[0]] * BITS)
+    lane_mix = weights([group[0]] * BITS, shrink(before + [group[2]] * 2))
     q_mix = weights(q_pairs(group[2], group[3]))
-    middle(1, got, out, buffer, before, diagonal[1:2, :], lane_mix, q_mix, group, True)
-
-
-def third_kernel(angles, diagonal, got, out, buffer):
+    middle(1, got, out, buffer, before, angles[1:2, :], lane_mix, q_mix, group, True)
+
+
+def third_kernel(angles, got, out, buffer):
     group = [pair_of(angles, 2, g) for g in range(4)]
-    q_mix = weights(q_pairs(group[2], group[3]))
-    row_mix = weights([group[1]] * BITS)
+    before = [pair_of(angles, 1, 1)] * BITS
+    q_mix = weights(q_pairs(group[2], group[3]), shrink(before + [group[2]] * 2))
+    row_mix = weights([group[1]] * BITS, shrink([group[0]] * BITS))
     lane = lax.broadcasted_iota(jnp.int32, (1, SIDE), 1)
-    own = jnp.where(lane == own_place(), diagonal[2:3, :], 0.0)
+    own = jnp.where(lane == own_place(), angles[2:3, :], 0.0)
     speed = jnp.sum(own, axis=1, keepdims=True)
-    before = [pair_of(angles, 1, 1)] * BITS
     middle(2, got, out, buffer, before, speed, q_mix, row_mix, group, False)
 
 
@@ -247,20 +258,21 @@
 
 def shards(wave_parts, level_table, diagonal_angles, turn_angles):
     wide, narrow = (SIDE * WIDE, SIDE), (SIDE * TILE, SIDE)
-    small = (turn_angles, diagonal_angles)
+    rest = SIDE - turn_angles.shape[1]
+    angles = jnp.concatenate([diagonal_angles, jnp.pad(turn_angles, ((0, 0), (0, rest)))])
     values = call(
         first_kernel,
         "first",
-        (*small, wave_parts, level_table),
-        [NEAR] * 4,
+        (angles, wave_parts, level_table),
+        [NEAR] * 3,
         wide,
     )
-    values = call(second_kernel, "second", (*small, exchange(values)), [NEAR] * 3, wide)
-    values = call(third_kernel, "third", (*small, exchange(values)), [NEAR] * 3, narrow)
+    values = call(second_kernel, "second", (angles, exchange(values)), [NEAR] * 2, wide)
+    values = call(third_kernel, "third", (angles, exchange(values)), [NEAR] * 2, narrow)
     return call(
         last_kernel,
         "last",
-        (turn_angles, exchange(values)),
+        (angles, exchange(values)),
         [NEAR] * 2,
         STATE,
         FAR,

time: 105 us -> 103 us (0.981)
  local copies, waits for them, and re-layouts: 3.35 us -> 1.99 us
    unnamed x8 -> x4, local copies, waits for them, and re-layouts: 3.35 us -> 1.99 us
where the time goes in v4:
time: 103 us
  blocking collectives  95.2 us (92%)
  Pallas kernels  5.22 us (5%)
  local copies, waits for them, and re-layouts  1.99 us (2%)
    all_to_all x3, blocking collectives, exchange(): lax.all_to_all(values.reshape(shape), ('qa', 'qb'), split_axis=0, concat_...  95.2 us
    pallas_call x4, Pallas kernels, call(): pl.pallas_call(kernel, name=name, in_specs=in_specs, out_specs=out_spec,...  5.22 us

profile of v4, /device:TPU:32, one launch (start us, length us, event | category | flops | bytes accessed | tf_op | source)
XLA Modules:
  0.0 103.1 jit_solution(2583157523278024395)
XLA Ops:
  0.0 0.7 select_maximum_fusion.angles
  0.7 0.0 copy-start
  0.7 1.0 %copy-done = f32[2,4,128,128]{3,2,1,0:T(8,128)S(1)} copy-done((f32[2,4,128,128]{3,2,1,0:T(8,128)S(1)}, f32[2,4,128,128]{3,2,1,0:T(8,128)}, u32[]{:S(2)}) %copy-start) | copy-done | bytes 524312
  1.7 0.0 copy-start.1
  1.8 0.9 copy-done.1
  2.7 1.1 %first.1 = f32[1536,128]{1,0:T(8,128)S(1)} custom-call(f32[6,128]{1,0:T(8,128)S(1)} %select_maximum_fusion.angles, f32[2,4,128,128]{3,2,1,0:T(8,128)S(1)} %copy-done, f32[4,128,128]{2,1,0:T(8,128)S(1)} %copy-done.1), custom_call_target="tpu_custom_call" | custom-call | tf_op jit(solution)/shard_map/first/pallas_call | solution.py:235
  3.8 40.5 %all_to_all.15 = f32[128,3,4,128]{3,2,1,0:T(4,128)S(1)} all-to-all(f32[128,3,4,128]{3,2,1,0:T(4,128)S(1)} %bitcast.11), channel_id=1, replica_groups=mesh['trial'=2,'qa'=16,'qb'=8] {'qa','qb'}, dimensions={0} | all-to-all | bytes 1572864 | tf_op jit(solution)/shard_map/all_to_all | solution.py:253
  44.3 1.4 %second.1 = f32[1536,128]{1,0:T(8,128)S(1)} custom-call(f32[6,128]{1,0:T(8,128)S(1)} %select_maximum_fusion.angles, f32[1536,128]{1,0:T(8,128)S(1)} %bitcast.8), custom_call_target="tpu_custom_call" | custom-call | tf_op jit(solution)/shard_map/second/pallas_call | solution.py:235
  45.7 30.6 %all_to_all.16 = f32[128,3,4,128]{3,2,1,0:T(4,128)S(1)} all-to-all(f32[128,3,4,128]{3,2,1,0:T(4,128)S(1)} %bitcast.9), channel_id=1, replica_groups=mesh['trial'=2,'qa'=16,'qb'=8] {'qa','qb'}, dimensions={0} | all-to-all | bytes 1572864 | tf_op jit(solution)/shard_map/all_to_all | solution.py:253
  76.3 1.4 %third.1 = f32[1024,128]{1,0:T(8,128)S(1)} custom-call(f32[6,128]{1,0:T(8,128)S(1)} %select_maximum_fusion.angles, f32[1536,128]{1,0:T(8,128)S(1)} %bitcast.10), custom_call_target="tpu_custom_call" | custom-call | tf_op jit(solution)/shard_map/third/pallas_call | solution.py:235
  77.7 24.1 %all_to_all.17 = f32[128,1,8,128]{3,2,1,0:T(8,128)S(1)} all-to-all(f32[128,1,8,128]{3,2,1,0:T(8,128)S(1)} %bitcast.13), channel_id=1, replica_groups=mesh['trial'=2,'qa'=16,'qb'=8] {'qa','qb'}, dimensions={0} | all-to-all | bytes 1048576 | tf_op jit(solution)/shard_map/all_to_all | solution.py:253
  101.7 1.4 %last.1 = f32[2,4,128,128]{3,2,1,0:T(8,128)} custom-call(f32[6,128]{1,0:T(8,128)S(1)} %select_maximum_fusion.angles, f32[1024,128]{1,0:T(8,128)S(1)} %bitcast.12), custom_call_target="tpu_custom_call" | custom-call | tf_op jit(solution)/shard_map/last/pallas_call | solution.py:235
Async XLA Ops:
  0.7 1.0 %copy-start = (f32[2,4,128,128]{3,2,1,0:T(8,128)S(1)}, f32[2,4,128,128]{3,2,1,0:T(8,128)}, u32[]{:S(2)}) copy-start(f32[2,4,128,128]{3,2,1,0:T(8,128)} %wave.1) | copy-start | bytes 1572868
  1.7 0.9 copy-start.1

commit v5 on v4

--- a/solution.py
+++ b/solution.py
@@ -6,7 +6,6 @@
 from jax.sharding import PartitionSpec as P
 
 SIDE = 128
-LAYERS = 3
 BITS = 7
 BLOCKS = 4
 PARTS = 2
@@ -35,8 +34,7 @@
 
 
 def pair_of(angles, layer, group):
-    row = LAYERS + layer
-    sine, cosine = sin_cos(jnp.broadcast_to(angles[row : row + 1, group : group + 1], (1, SIDE)))
+    sine, cosine = sin_cos(jnp.broadcast_to(angles[layer : layer + 1, group : group + 1], (1, SIDE)))
     return sine, cosine, sine / cosine
 
 
@@ -138,14 +136,36 @@
     return store
 
 
-def first_kernel(angles, wave, levels, out, buffer):
+def first_kernel(
+    angles_far, diagonal_far, wave_far, levels_far, out, buffer, angles, diagonal, wave, levels, sems
+):
+    def copies(b):
+        return [
+            pltpu.make_async_copy(levels_far.at[b], levels.at[b], sems.at[0, b]),
+            pltpu.make_async_copy(wave_far.at[0, b], wave.at[0, b], sems.at[1, b]),
+            pltpu.make_async_copy(wave_far.at[1, b], wave.at[1, b], sems.at[2, b]),
+        ]
+
+    small = [
+        pltpu.make_async_copy(angles_far, angles, sems.at[3, 0]),
+        pltpu.make_async_copy(diagonal_far, diagonal, sems.at[3, 1]),
+    ]
+    for copy in small:
+        copy.start()
+    for b in range(BLOCKS):
+        for copy in copies(b):
+            copy.start()
+    for copy in small:
+        copy.wait()
     group = [pair_of(angles, 0, g) for g in range(4)]
     after = [group[1]] * BITS
     lane_mix = weights([group[0]] * BITS, shrink(after + [group[2]] * 2))
     count = bit_counts(own_place())
-    speed = angles[0:1, :]
+    speed = diagonal[0:1, :]
     real, imag = [], []
     for b in range(BLOCKS):
+        for copy in copies(b):
+            copy.wait()
         level = levels[b]
         sine, cosine = sin_cos(level * speed, count + b.bit_count())
         r, i = turned(wave[0, b], wave[1, b], sine, cosine)
@@ -184,21 +204,21 @@
     return [qb_pair] * QB_BITS + [qa_pair] * (BITS - QB_BITS)
 
 
-def second_kernel(angles, got, out, buffer):
+def second_kernel(angles, diagonal, got, out, buffer):
     before = q_pairs(pair_of(angles, 0, 2), pair_of(angles, 0, 3))
     group = [pair_of(angles, 1, g) for g in range(4)]
     lane_mix = weights([group[0]] * BITS, shrink(before + [group[2]] * 2))
     q_mix = weights(q_pairs(group[2], group[3]))
-    middle(1, got, out, buffer, before, angles[1:2, :], lane_mix, q_mix, group, True)
-
-
-def third_kernel(angles, got, out, buffer):
+    middle(1, got, out, buffer, before, diagonal[1:2, :], lane_mix, q_mix, group, True)
+
+
+def third_kernel(angles, diagonal, got, out, buffer):
     group = [pair_of(angles, 2, g) for g in range(4)]
     before = [pair_of(angles, 1, 1)] * BITS
     q_mix = weights(q_pairs(group[2], group[3]), shrink(before + [group[2]] * 2))
     row_mix = weights([group[1]] * BITS, shrink([group[0]] * BITS))
     lane = lax.broadcasted_iota(jnp.int32, (1, SIDE), 1)
-    own = jnp.where(lane == own_place(), angles[2:3, :], 0.0)
+    own = jnp.where(lane == own_place(), diagonal[2:3, :], 0.0)
     speed = jnp.sum(own, axis=1, keepdims=True)
     middle(2, got, out, buffer, before, speed, q_mix, row_mix, group, False)
 
@@ -231,7 +251,7 @@
 STATE = (PARTS, BLOCKS, SIDE, SIDE)
 
 
-def call(kernel, name, operands, in_specs, out_shape, out_spec=NEAR, scratch=()):
+def call(kernel, name, operands, in_specs, out_shape, out_spec=NEAR, scratch=(), grant=32 << 20):
     return pl.pallas_call(
         kernel,
         name=name,
@@ -239,7 +259,7 @@
         out_specs=out_spec,
         out_shape=jax.ShapeDtypeStruct(out_shape, jnp.float32),
         scratch_shapes=[pltpu.VMEM((SIDE * TILE, SIDE), jnp.float32), *scratch],
-        compiler_params=pltpu.CompilerParams(vmem_limit_bytes=32 * 1024 * 1024),
+        compiler_params=pltpu.CompilerParams(vmem_limit_bytes=grant),
         interpret=INTERPRET,
     )(*operands)
 
@@ -258,17 +278,24 @@
 
 def shards(wave_parts, level_table, diagonal_angles, turn_angles):
     wide, narrow = (SIDE * WIDE, SIDE), (SIDE * TILE, SIDE)
-    rest = SIDE - turn_angles.shape[1]
-    angles = jnp.concatenate([diagonal_angles, jnp.pad(turn_angles, ((0, 0), (0, rest)))])
+    angles, small = turn_angles, (turn_angles, diagonal_angles)
     values = call(
         first_kernel,
         "first",
-        (angles, wave_parts, level_table),
-        [NEAR] * 3,
+        (*small, wave_parts, level_table),
+        [FAR] * 4,
         wide,
-    )
-    values = call(second_kernel, "second", (angles, exchange(values)), [NEAR] * 2, wide)
-    values = call(third_kernel, "third", (angles, exchange(values)), [NEAR] * 2, narrow)
+        scratch=[
+            pltpu.VMEM(turn_angles.shape, jnp.float32),
+            pltpu.VMEM(diagonal_angles.shape, jnp.float32),
+            pltpu.VMEM(STATE, jnp.float32),
+            pltpu.VMEM(STATE[1:], jnp.float32),
+            pltpu.SemaphoreType.DMA((4, BLOCKS)),
+        ],
+        grant=56 << 20,
+    )
+    values = call(second_kernel, "second", (*small, exchange(values)), [NEAR] * 3, wide)
+    values = call(third_kernel, "third", (*small, exchange(values)), [NEAR] * 3, narrow)
     return call(
         last_kernel,
         "last",

time: 103 us -> 103 us (level)
  local copies, waits for them, and re-layouts: 1.99 us -> 0.01 us
  Pallas kernels: 5.22 us -> 7.07 us
    unnamed x4, local copies, waits for them, and re-layouts: 1.99 us -> 0.01 us
    pallas_call x4, Pallas kernels: 5.22 us -> 7.07 us  [call(): pl.pallas_call(kernel, name=name, in_specs=in_specs, out_specs=out_spec,...]
where the time goes in v5:
time: 103 us; the launch traced here: 102 us
  blocking collectives  95.3 us (93%)
  Pallas kernels  7.07 us (7%)
    all_to_all x3, blocking collectives, exchange(): lax.all_to_all(values.reshape(shape), ('qa', 'qb'), split_axis=0, concat_...  95.3 us
    pallas_call x4, Pallas kernels, call(): pl.pallas_call(kernel, name=name, in_specs=in_specs, out_specs=out_spec,...  7.07 us

profile of v5, /device:TPU:32, one launch (start us, length us, event | category | flops | bytes accessed | tf_op | source)
XLA Modules:
  0.0 102.4 jit_solution(9410697108171405936)
XLA Ops:
  0.0 3.0 %first.1 = f32[1536,128]{1,0:T(8,128)} custom-call(f32[3,4]{1,0:T(4,128)} %angles.5, f32[3,128]{1,0:T(4,128)} %diagonal.3, f32[2,4,128,128]{3,2,1,0:T(8,128)} %wave_far.1, f32[4,128,128]{2,1,0:T(8,128)} %levels_far.1), custom_call_target="tpu_custom_call" | custom-call | tf_op jit(solution)/shard_map/first/pallas_call | solution.py:255
  3.0 0.0 copy-start
  3.0 0.0 copy-start.1
  3.0 40.7 %all_to_all.15 = f32[128,3,4,128]{3,2,1,0:T(4,128)S(1)} all-to-all(f32[128,3,4,128]{3,2,1,0:T(4,128)} %bitcast.13), channel_id=1, replica_groups=mesh['trial'=2,'qa'=16,'qb'=8] {'qa','qb'}, dimensions={0} | all-to-all | bytes 1572864 | tf_op jit(solution)/shard_map/all_to_all | solution.py:273
  43.7 0.0 copy-done
  43.7 0.0 copy-done.1
  43.7 1.4 %second.1 = f32[1536,128]{1,0:T(8,128)S(1)} custom-call(f32[3,4]{1,0:T(4,128)S(1)} %copy-done, f32[3,128]{1,0:T(4,128)S(1)} %copy-done.1, f32[1536,128]{1,0:T(8,128)S(1)} %bitcast.8), custom_call_target="tpu_custom_call" | custom-call | tf_op jit(solution)/shard_map/second/pallas_call | solution.py:255
  45.0 30.6 %all_to_all.16 = f32[128,3,4,128]{3,2,1,0:T(4,128)S(1)} all-to-all(f32[128,3,4,128]{3,2,1,0:T(4,128)S(1)} %bitcast.9), channel_id=1, replica_groups=mesh['trial'=2,'qa'=16,'qb'=8] {'qa','qb'}, dimensions={0} | all-to-all | bytes 1572864 | tf_op jit(solution)/shard_map/all_to_all | solution.py:273
  75.7 1.4 %third.1 = f32[1024,128]{1,0:T(8,128)S(1)} custom-call(f32[3,4]{1,0:T(4,128)S(1)} %copy-done, f32[3,128]{1,0:T(4,128)S(1)} %copy-done.1, f32[1536,128]{1,0:T(8,128)S(1)} %bitcast.10), custom_call_target="tpu_custom_call" | custom-call | tf_op jit(solution)/shard_map/third/pallas_call | solution.py:255
  77.1 24.0 %all_to_all.17 = f32[128,1,8,128]{3,2,1,0:T(8,128)S(1)} all-to-all(f32[128,1,8,128]{3,2,1,0:T(8,128)S(1)} %bitcast.11), channel_id=1, replica_groups=mesh['trial'=2,'qa'=16,'qb'=8] {'qa','qb'}, dimensions={0} | all-to-all | bytes 1048576 | tf_op jit(solution)/shard_map/all_to_all | solution.py:273
  101.1 1.4 %last.1 = f32[2,4,128,128]{3,2,1,0:T(8,128)} custom-call(f32[3,4]{1,0:T(4,128)S(1)} %copy-done, f32[1024,128]{1,0:T(8,128)S(1)} %bitcast.12), custom_call_target="tpu_custom_call" | custom-call | tf_op jit(solution)/shard_map/last/pallas_call | solution.py:255
Async XLA Ops:
  3.0 40.7 %copy-start = (f32[3,4]{1,0:T(4,128)S(1)}, f32[3,4]{1,0:T(4,128)}, u32[]{:S(2)}) copy-start(f32[3,4]{1,0:T(4,128)} %angles.5) | copy-start | bytes 148
  3.0 40.7 %copy-start.1 = (f32[3,128]{1,0:T(4,128)S(1)}, f32[3,128]{1,0:T(4,128)}, u32[]{:S(2)}) copy-start(f32[3,128]{1,0:T(4,128)} %diagonal.3) | copy-start | bytes 4612

commit v6 on v5

--- a/solution.py
+++ b/solution.py
@@ -57,14 +57,16 @@
     return product
 
 
-def mix_tiles(load, store, pairs):
-    for high in range(0, SIDE, 8):
-        for i, value in enumerate(butterfly([load(high + i) for i in range(8)], pairs[:3])):
-            store(high + i, value, 0)
+def mix_tiles(load, store, pairs, done=lambda end: None):
     for low in range(8):
         order = range(low, SIDE, 8)
-        for i, value in zip(order, butterfly([store(i, None, 0) for i in order], pairs[3:])):
-            store(i, value, 1)
+        for i, value in zip(order, butterfly([load(i) for i in order], pairs[3:])):
+            store(i, value, 0)
+    for high in range(0, SIDE, 8):
+        values = [store(high + i, None, 0) for i in range(8)]
+        for i, value in enumerate(butterfly(values, pairs[:3])):
+            store(high + i, value, 1)
+        done(high + 8)
 
 
 def weights(pairs, scale=1.0):
@@ -137,7 +139,7 @@
 
 
 def first_kernel(
-    angles_far, diagonal_far, wave_far, levels_far, out, buffer, angles, diagonal, wave, levels, sems
+    angles_far, diagonal_far, wave_far, levels_far, out_far, buffer, angles, diagonal, wave, levels, out, sems
 ):
     def copies(b):
         return [
@@ -176,7 +178,18 @@
         for b in range(BLOCKS):
             buffer[every(TILE, p * BLOCKS + b), :] = mix_lanes(part[b], lane_mix)
     store = in_buffer(buffer, out, WIDE)
-    mix_tiles(lambda i: store(i, None, 0), store, after)
+    quarter, leaving = SIDE // 4, []
+
+    def done(end):
+        if end % quarter == 0:
+            rows = pl.ds(WIDE * (end - quarter), WIDE * quarter)
+            copy = pltpu.make_async_copy(out.at[rows], out_far.at[rows], sems.at[4, end // quarter - 1])
+            copy.start()
+            leaving.append(copy)
+
+    mix_tiles(lambda i: store(i, None, 0), store, after, done)
+    for copy in leaving:
+        copy.wait()
 
 
 def middle(layer, got, out, buffer, before, speed, lane_mix, next_mix, group, send_levels):
@@ -285,12 +298,14 @@
         (*small, wave_parts, level_table),
         [FAR] * 4,
         wide,
+        FAR,
         scratch=[
             pltpu.VMEM(turn_angles.shape, jnp.float32),
             pltpu.VMEM(diagonal_angles.shape, jnp.float32),
             pltpu.VMEM(STATE, jnp.float32),
             pltpu.VMEM(STATE[1:], jnp.float32),
-            pltpu.SemaphoreType.DMA((4, BLOCKS)),
+            pltpu.VMEM(wide, jnp.float32),
+            pltpu.SemaphoreType.DMA((5, BLOCKS)),
         ],
         grant=56 << 20,
     )

time: 103 us -> 103 us (level)
  no operation moved by 1% of the time
where the time goes in v6:
time: 103 us; the launch traced here: 102 us
  blocking collectives  95.3 us (93%)
  Pallas kernels  7.05 us (7%)
    all_to_all x3, blocking collectives, exchange(): lax.all_to_all(values.reshape(shape), ('qa', 'qb'), split_axis=0, concat_...  95.3 us
    pallas_call x4, Pallas kernels, call(): pl.pallas_call(kernel, name=name, in_specs=in_specs, out_specs=out_spec,...  7.05 us

profile of v6, /device:TPU:32, one launch (start us, length us, event | category | flops | bytes accessed | tf_op | source)
XLA Modules:
  0.0 102.4 jit_solution(91605796821521548)
XLA Ops:
  0.0 2.9 %first.1 = f32[1536,128]{1,0:T(8,128)} custom-call(f32[3,4]{1,0:T(4,128)} %angles.5, f32[3,128]{1,0:T(4,128)} %diagonal.3, f32[2,4,128,128]{3,2,1,0:T(8,128)} %wave_far.1, f32[4,128,128]{2,1,0:T(8,128)} %levels_far.1), custom_call_target="tpu_custom_call" | custom-call | tf_op jit(solution)/shard_map/first/pallas_call | solution.py:268
  2.9 0.0 copy-start
  2.9 0.0 copy-start.1
  2.9 40.7 %all_to_all.15 = f32[128,3,4,128]{3,2,1,0:T(4,128)S(1)} all-to-all(f32[128,3,4,128]{3,2,1,0:T(4,128)} %bitcast.13), channel_id=1, replica_groups=mesh['trial'=2,'qa'=16,'qb'=8] {'qa','qb'}, dimensions={0} | all-to-all | bytes 1572864 | tf_op jit(solution)/shard_map/all_to_all | solution.py:286
  43.6 0.0 copy-done
  43.6 0.0 copy-done.1
  43.7 1.4 %second.1 = f32[1536,128]{1,0:T(8,128)S(1)} custom-call(f32[3,4]{1,0:T(4,128)S(1)} %copy-done, f32[3,128]{1,0:T(4,128)S(1)} %copy-done.1, f32[1536,128]{1,0:T(8,128)S(1)} %bitcast.8), custom_call_target="tpu_custom_call" | custom-call | tf_op jit(solution)/shard_map/second/pallas_call | solution.py:268
  45.0 30.6 %all_to_all.16 = f32[128,3,4,128]{3,2,1,0:T(4,128)S(1)} all-to-all(f32[128,3,4,128]{3,2,1,0:T(4,128)S(1)} %bitcast.9), channel_id=1, replica_groups=mesh['trial'=2,'qa'=16,'qb'=8] {'qa','qb'}, dimensions={0} | all-to-all | bytes 1572864 | tf_op jit(solution)/shard_map/all_to_all | solution.py:286
  75.6 1.4 %third.1 = f32[1024,128]{1,0:T(8,128)S(1)} custom-call(f32[3,4]{1,0:T(4,128)S(1)} %copy-done, f32[3,128]{1,0:T(4,128)S(1)} %copy-done.1, f32[1536,128]{1,0:T(8,128)S(1)} %bitcast.10), custom_call_target="tpu_custom_call" | custom-call | tf_op jit(solution)/shard_map/third/pallas_call | solution.py:268
  77.0 24.1 %all_to_all.17 = f32[128,1,8,128]{3,2,1,0:T(8,128)S(1)} all-to-all(f32[128,1,8,128]{3,2,1,0:T(8,128)S(1)} %bitcast.11), channel_id=1, replica_groups=mesh['trial'=2,'qa'=16,'qb'=8] {'qa','qb'}, dimensions={0} | all-to-all | bytes 1048576 | tf_op jit(solution)/shard_map/all_to_all | solution.py:286
  101.0 1.4 %last.1 = f32[2,4,128,128]{3,2,1,0:T(8,128)} custom-call(f32[3,4]{1,0:T(4,128)S(1)} %copy-done, f32[1024,128]{1,0:T(8,128)S(1)} %bitcast.12), custom_call_target="tpu_custom_call" | custom-call | tf_op jit(solution)/shard_map/last/pallas_call | solution.py:268
Async XLA Ops:
  2.9 40.7 %copy-start = (f32[3,4]{1,0:T(4,128)S(1)}, f32[3,4]{1,0:T(4,128)}, u32[]{:S(2)}) copy-start(f32[3,4]{1,0:T(4,128)} %angles.5) | copy-start | bytes 148
  2.9 40.7 %copy-start.1 = (f32[3,128]{1,0:T(4,128)S(1)}, f32[3,128]{1,0:T(4,128)}, u32[]{:S(2)}) copy-start(f32[3,128]{1,0:T(4,128)} %diagonal.3) | copy-start | bytes 4612
